TPU v7x, 32 devices: a whole 2x2x4 slice. The times are simulated.
32 devices in a mesh: gz: 8 (over z, y), ga: 4 (over x, core).
Axes of the slice: x: 2, y: 2, z: 4, core: 2. Of those that a mesh axis runs over, the one named last changes fastest.
Arguments:
- solution: float32 [64, 256, 256], P(('gz', 'ga')), may hold values from -6 to 6
- residual: float32 [64, 256, 256], P(('gz', 'ga')), may hold values from -40 to 40
- direction: float32 [64, 256, 256], P(('gz', 'ga')), may hold values from -40 to 40
Outputs:
- solution_out: float32 [64, 256, 256], P(('gz', 'ga'))
- residual_out: float32 [64, 256, 256], P(('gz', 'ga'))
- direction_out: float32 [64, 256, 256], P(('gz', 'ga'))
All inputs are finite; a program needn't handle non-finite values.
Results may differ from a plain program's by a relative error of at most 0.0003.
Values sent between devices are 32-bit elements; how exact they have to be, the bound alone decides.
A program may use at most 128 MiB of HBM per device.

v0:
```python
import functools

import jax
import jax.numpy as jnp
import numpy as np
from jax import lax
from jax.experimental import pallas as pl
from jax.experimental.pallas import tpu as pltpu
from jax.sharding import PartitionSpec as P

S = 8
MESH = pl.DeviceIdType.MESH
first_scale = -1.0 / 6.0
next_scale = -1.0 / 3.0
SIDE = 24
LANES = 128


def change_matrix(steps):
    count = 2 * steps + 1
    table = np.zeros((count, count), np.float64)
    for offset, length in ((0, steps + 1), (steps + 1, steps)):
        for power in range(length - 1):
            column = offset + power
            table[column, column] = 6.0
            if power == 0:
                table[column + 1, column] = 6.0
            else:
                table[column + 1, column] = 3.0
                table[column - 1, column] = 3.0
    return table


def dd(power, odd):
    return 2 * power + odd


def rr(power, odd):
    return 2 * S + 1 + 2 * power + odd


def dr(power, odd):
    return 4 * S + 2 * power + odd


COUNT = 6 * S


def gram_tables():
    def moment(kind, order):
        half, odd = order // 2, order % 2
        row = np.zeros(COUNT)
        row[kind(half, odd)] += 2.0
        row[kind(0, odd)] -= 1.0
        return row

    size = 2 * S + 1
    table = np.zeros((COUNT, size, size))
    for i in range(size):
        for j in range(size):
            a, b = (i if i <= S else i - S - 1), (j if j <= S else j - S - 1)
            kind = dd if (i <= S and j <= S) else rr if (i > S and j > S) else dr
            table[:, i, j] = 0.5 * (moment(kind, a + b) + moment(kind, abs(a - b)))
    moved = table @ change_matrix(S)

    def padded(t):
        out = np.zeros((t.shape[0], SIDE, LANES), np.float32)
        out[:, :size, :size] = t
        return out

    change = np.stack([change_matrix(S), change_matrix(S).T])
    return padded(table), padded(moved), padded(change)


def kernel(gz_count, ga, res_ref, dir_ref, gram_hbm, moved_hbm, change_tab,
           fin,
           X, halo, stage, accs, red1, red2, coef, outbuf, held, gram_tab, moved_tab,
           in_send, in_recv, own_sem, z_send, z_recv, r_send, r_recv,
           a_send, a_recv, b_send, b_recv, o_send, o_recv, load_sem):
    group = 2 * ga
    groups = gz_count // 2
    planes, width, depth = res_ref.shape
    tall = planes * group
    rows = width // group
    iz, ia = lax.axis_index("gz"), lax.axis_index("ga")
    g = iz // 2
    p = (iz % 2) * ga + ia

    def place(position):
        upper = position // ga
        return upper * (3 * ga - 1 - position) + (1 - upper) * position

    b = place(p)

    def device(which, position):
        return (which * 2 + position // ga, position % ga)

    def block_rows(block):
        return pl.ds(pl.multiple_of(block * rows, rows), rows)

    loads = [pltpu.make_async_copy(source, target, load_sem.at[i]) for i, (source, target) in enumerate((
        (dir_ref, held.at[0]), (res_ref, held.at[1]), (gram_hbm, gram_tab), (moved_hbm, moved_tab)))]
    for load in loads:
        load.start()

    barrier = pltpu.get_barrier_semaphore()
    for j in range(1, group):
        pl.semaphore_signal(barrier, inc=1, device_id=device(g, (p + j) % group), device_id_type=MESH)
    for j in range(1, groups):
        pl.semaphore_signal(barrier, inc=1, device_id=device((g + j) % groups, p), device_id_type=MESH)
    pl.semaphore_wait(barrier, group - 1 + groups - 1)

    def incoming(c, j):
        q = (p + j) % group
        return pltpu.make_async_remote_copy(
            src_ref=held.at[c, :, block_rows(place(q)), :],
            dst_ref=X.at[c, 0, pl.ds(1 + planes * p, planes)],
            send_sem=in_send.at[c, j], recv_sem=in_recv.at[c, j],
            device_id=device(g, q), device_id_type=MESH)

    def own_in(c):
        return pltpu.make_async_copy(
            held.at[c, :, block_rows(b), :],
            X.at[c, 0, pl.ds(1 + planes * p, planes)], own_sem.at[c])

    for c in range(2):
        loads[c].wait()
        for j in range(1, group):
            incoming(c, j).start()
        own_in(c).start()

    below, above = g > 0, g < groups - 1
    before, after = b > 0, b < group - 1

    @pl.when(g == 0)
    def _():
        for c in range(2):
            for k in range(S):
                X[c, k, 0] = jnp.zeros((rows, depth), jnp.float32)

    @pl.when(g == groups - 1)
    def _():
        for c in range(2):
            for k in range(S):
                X[c, k, tall + 1] = jnp.zeros((rows, depth), jnp.float32)

    @pl.when(b == 0)
    def _():
        for c in range(2):
            for k in range(S):
                halo[c, k, 0] = jnp.zeros((tall, depth), jnp.float32)

    @pl.when(b == group - 1)
    def _():
        for c in range(2):
            for k in range(S):
                halo[c, k, 1] = jnp.zeros((tall, depth), jnp.float32)

    def z_copy(c, k, up):
        return pltpu.make_async_remote_copy(
            src_ref=X.at[c, k, tall if up else 1],
            dst_ref=X.at[c, k, 0 if up else tall + 1],
            send_sem=z_send.at[c, k, up], recv_sem=z_recv.at[c, k, up],
            device_id=device(g + (1 if up else -1), p), device_id_type=MESH)

    def r_copy(c, k, up):
        return pltpu.make_async_remote_copy(
            src_ref=stage.at[c, k, up],
            dst_ref=halo.at[c, k, 1 - up],
            send_sem=r_send.at[c, k, up], recv_sem=r_recv.at[c, k, up],
            device_id=device(g, place(b + (1 if up else -1))), device_id_type=MESH)

    def send_z(c, k):
        @pl.when(below)
        def _():
            z_copy(c, k, 0).start()

        @pl.when(above)
        def _():
            z_copy(c, k, 1).start()

    def send_rows(c, k):
        @pl.when(before)
        def _():
            r_copy(c, k, 0).start()

        @pl.when(after)
        def _():
            r_copy(c, k, 1).start()

    def receive(c, k):
        @pl.when(before)
        def _():
            r_copy(c, k, 1).wait_recv()

        @pl.when(after)
        def _():
            r_copy(c, k, 0).wait_recv()

        @pl.when(below)
        def _():
            z_copy(c, k, 1).wait_recv()

        @pl.when(above)
        def _():
            z_copy(c, k, 0).wait_recv()

    row_ids = lax.broadcasted_iota(jnp.int32, (rows, depth), 0)
    col_ids = lax.broadcasted_iota(jnp.int32, (rows, depth), 1)
    first_row, last_row = row_ids == 0, row_ids == rows - 1
    first_col, last_col = col_ids == 0, col_ids == depth - 1

    def folded(x):
        total = x[0:8]
        for i in range(8, rows, 8):
            total = total + x[i:i + 8]
        out = total[:, 0:LANES]
        for i in range(LANES, depth, LANES):
            out = out + total[:, i:i + LANES]
        return out

    def chain_step(c, k):
        if c == 0:
            names = [(dd(k, 0), "new", "new"), (dd(k - 1, 1), "new", "cur")]
            if k == 1:
                names.append((dd(0, 0), "cur", "cur"))
        else:
            names = [(rr(k, 0), "new", "new"), (rr(k - 1, 1), "new", "cur"),
                     (dr(k, 0), "new", "other"), (dr(k - 1, 1), "cur", "other")]
            if k == S - 1:
                names.append((dr(k, 1), "new", "ahead"))
            if k == 1:
                names += [(rr(0, 0), "cur", "cur"), (dr(0, 0), "cur", "start")]

        def plane(z, sums):
            cur = X[c, k - 1, z + 1]
            total = X[c, k - 1, z] + X[c, k - 1, z + 2]
            low = halo[c, k - 1, 0, pl.ds(z, 1), :]
            high = halo[c, k - 1, 1, pl.ds(z, 1), :]
            total = total + jnp.where(first_row, low, pltpu.roll(cur, 1, 0))
            total = total + jnp.where(last_row, high, pltpu.roll(cur, rows - 1, 0))
            total = total + jnp.where(first_col, 0.0, pltpu.roll(cur, 1, 1))
            total = total + jnp.where(last_col, 0.0, pltpu.roll(cur, depth - 1, 1))
            if k == 1:
                new = total * first_scale
            else:
                new = total * next_scale - X[c, k - 2, z + 1]
            X[c, k, z + 1] = new
            if k < (S if c == 0 else S - 1):
                stage[c, k, 0, pl.ds(z, 1), :] = new[0:1]
                stage[c, k, 1, pl.ds(z, 1), :] = new[rows - 1:rows]
            have = {"new": new, "cur": cur}
            if any("other" in n for n in names):
                have["other"] = X[0, k, z + 1]
            if any("ahead" in n for n in names):
                have["ahead"] = X[0, k + 1, z + 1]
            if any("start" in n for n in names):
                have["start"] = X[0, 0, z + 1]
            return tuple(s + folded(have[l] * have[r]) for s, (_, l, r) in zip(sums, names))

        more = k < (S if c == 0 else S - 1)
        sums = tuple(jnp.zeros((8, LANES), jnp.float32) for _ in names)
        sums = plane(0, sums)
        sums = plane(tall - 1, sums)
        if more:
            send_z(c, k)
        sums = lax.fori_loop(1, tall - 1, plane, sums, unroll=7)
        if more:
            send_rows(c, k)
        for s, (slot, _, _) in zip(sums, names):
            accs[slot] = s

    def arrive(c):
        own_in(c).wait()
        for j in range(1, group):
            incoming(c, j).wait_recv()
        send_z(c, 0)
        for z in range(tall):
            stage[c, 0, 0, z:z + 1, :] = X[c, 0, z + 1, 0:1, :]
            stage[c, 0, 1, z:z + 1, :] = X[c, 0, z + 1, rows - 1:rows, :]
        send_rows(c, 0)

    arrive(0)
    receive(0, 0)
    chain_step(0, 1)
    receive(0, 1)
    chain_step(0, 2)
    arrive(1)
    for k in range(1, S):
        receive(1, k - 1)
        chain_step(1, k)
        if k + 2 <= S:
            receive(0, k + 1)
            chain_step(0, k + 2)

    lanes = lax.broadcasted_iota(jnp.int32, (8, LANES), 1)
    packed = jnp.zeros((8, LANES), jnp.float32)
    for t in range(COUNT // 8):
        part = jnp.sum(jnp.sum(accs[8 * t:8 * t + 8], axis=1), axis=1, keepdims=True)
        packed = packed + jnp.where(lanes == t, part, 0.0)
    red1[p] = packed

    def first_sum(j, mine):
        q = (p + j) % group
        slot = p if mine else q
        return pltpu.make_async_remote_copy(
            src_ref=red1.at[p], dst_ref=red1.at[slot],
            send_sem=a_send.at[j], recv_sem=a_recv.at[slot],
            device_id=device(g, q), device_id_type=MESH)

    def second_sum(j, mine):
        q = (g + j) % groups
        slot = g if mine else q
        return pltpu.make_async_remote_copy(
            src_ref=red2.at[g], dst_ref=red2.at[slot],
            send_sem=b_send.at[j], recv_sem=b_recv.at[slot],
            device_id=device(q, p), device_id_type=MESH)

    for j in range(1, group):
        first_sum(j, True).start()
    for j in range(1, group):
        first_sum(j, False).wait_recv()
    total = red1[0]
    for i in range(1, group):
        total = total + red1[i]
    red2[g] = total
    for j in range(1, groups):
        second_sum(j, True).start()
    for j in range(1, groups):
        second_sum(j, False).wait_recv()
    total = red2[0]
    for i in range(1, groups):
        total = total + red2[i]

    loads[2].wait()
    loads[3].wait()
    gram = jnp.zeros((SIDE, LANES), jnp.float32)
    moved = jnp.zeros((SIDE, LANES), jnp.float32)
    for e in range(COUNT):
        value = total[e % 8:e % 8 + 1, e // 8:e // 8 + 1]
        gram = gram + value * gram_tab[e]
        moved = moved + value * moved_tab[e]
    change, change_t = change_tab[0], change_tab[1]

    def full(x):
        return jnp.sum(jnp.sum(x, axis=0, keepdims=True), axis=1, keepdims=True)

    def unit(axis, at):
        ids = lax.broadcasted_iota(jnp.int32, (SIDE, LANES), axis)
        return jnp.where(ids == at, 1.0, 0.0).astype(jnp.float32)

    def inner(_, state):
        qc, qr, wc, wr, it, rho = state
        alpha = rho / full(qc * (moved * qr))
        mc = jnp.sum(change * qr, axis=1, keepdims=True)
        mr = jnp.sum(change_t * qc, axis=0, keepdims=True)
        it = it + alpha * qc
        wc = wc - alpha * mc
        wr = wr - alpha * mr
        rho_new = full(wc * (gram * wr))
        beta = rho_new / rho
        return wc + beta * qc, wr + beta * qr, wc, wr, it, rho_new

    wc, wr = unit(0, S + 1), unit(1, S + 1)
    state = (unit(0, 0), unit(1, 0), wc, wr, jnp.zeros((SIDE, LANES), jnp.float32),
             full(wc * (gram * wr)))
    qc, qr, wc, wr, it, rho = lax.fori_loop(0, S, inner, state)
    coef[0] = it
    coef[1] = wc
    coef[2] = qc

    def outgoing(j):
        q = (p + j) % group
        return pltpu.make_async_remote_copy(
            src_ref=outbuf.at[q],
            dst_ref=fin.at[:, :, block_rows(b), :],
            send_sem=o_send.at[j], recv_sem=o_recv.at[j],
            device_id=device(g, q), device_id_type=MESH)

    def outgoing_from(j):
        q = (p + group - j) % group
        return pltpu.make_async_remote_copy(
            src_ref=outbuf.at[q],
            dst_ref=fin.at[:, :, block_rows(place(q)), :],
            send_sem=o_send.at[j], recv_sem=o_recv.at[j],
            device_id=device(g, q), device_id_type=MESH)

    def combine(q):
        for i in range(planes):
            def strip(s, carry):
                at = pl.ds(pl.multiple_of(s * 16, 16), 16)
                sums = [None, None, None]
                for v in range(2 * S + 1):
                    c, k = (0, v) if v <= S else (1, v - S - 1)
                    x = X[c, k, planes * q + i + 1, at, :]
                    for o in range(3):
                        f = coef[o, v:v + 1, :]
                        f = jnp.concatenate([f] * (depth // LANES), axis=1)
                        term = f * x
                        sums[o] = term if sums[o] is None else sums[o] + term
                for o in range(3):
                    outbuf[q, o, i, at, :] = sums[o]
                return carry
            lax.fori_loop(0, rows // 16, strip, 0)

    for j in range(1, group):
        combine((p + j) % group)
        outgoing(j).start()
    combine(p)
    own_out = pltpu.make_async_copy(outbuf.at[p], fin.at[:, :, block_rows(b), :], own_sem.at[2])
    own_out.start()
    own_out.wait()
    for j in range(1, group):
        outgoing_from(j).wait_recv()

    for c in range(2):
        for j in range(1, group):
            incoming(c, j).wait_send()
        for k in range(S if c == 0 else S - 1):
            @pl.when(below)
            def _():
                z_copy(c, k, 0).wait_send()

            @pl.when(above)
            def _():
                z_copy(c, k, 1).wait_send()

            @pl.when(before)
            def _():
                r_copy(c, k, 0).wait_send()

            @pl.when(after)
            def _():
                r_copy(c, k, 1).wait_send()
    for j in range(1, group):
        first_sum(j, True).wait_send()
        outgoing(j).wait_send()
    for j in range(1, groups):
        second_sum(j, True).wait_send()


def on_device(gz_count, ga, sol, res, direction):
    planes, width, depth = sol.shape
    group, groups = 2 * ga, gz_count // 2
    tall, rows = planes * group, width // group
    gram_tab, moved_tab, change_tab = (jnp.asarray(t) for t in gram_tables())
    vmem = pl.BlockSpec(memory_space=pltpu.VMEM)
    dma = pltpu.SemaphoreType.DMA
    shape = jax.ShapeDtypeStruct((3,) + sol.shape, jnp.float32)
    anywhere = pl.BlockSpec(memory_space=pl.ANY)
    f32 = jnp.float32
    combined = pl.pallas_call(
        functools.partial(kernel, gz_count, ga),
        out_shape=shape,
        in_specs=[anywhere] * 4 + [vmem],
        out_specs=vmem,
        scratch_shapes=[
            pltpu.VMEM((2, S + 1, tall + 2, rows, depth), f32),
            pltpu.VMEM((2, S, 2, tall, depth), f32),
            pltpu.VMEM((2, S, 2, tall, depth), f32),
            pltpu.VMEM((COUNT, 8, LANES), f32),
            pltpu.VMEM((group, 8, LANES), f32),
            pltpu.VMEM((groups, 8, LANES), f32),
            pltpu.VMEM((3, SIDE, LANES), f32),
            pltpu.VMEM((group, 3, planes, rows, depth), f32),
            pltpu.VMEM((2, planes, width, depth), f32),
            pltpu.VMEM((COUNT, SIDE, LANES), f32),
            pltpu.VMEM((COUNT, SIDE, LANES), f32),
            dma((2, group)), dma((2, group)), dma((3,)),
            dma((2, S, 2)), dma((2, S, 2)), dma((2, S, 2)), dma((2, S, 2)),
            dma((group,)), dma((group,)), dma((groups,)), dma((groups,)),
            dma((group,)), dma((group,)), dma((4,)),
        ],
        compiler_params=pltpu.CompilerParams(collective_id=0, has_side_effects=True),
    )(res, direction, gram_tab, moved_tab, change_tab)
    return sol + combined[0], combined[1], combined[2]


def solution(mesh):
    spec = P(("gz", "ga"), None, None)
    return jax.shard_map(
        functools.partial(on_device, mesh.shape["gz"], mesh.shape["ga"]),
        mesh=mesh, in_specs=(spec, spec, spec), out_specs=(spec, spec, spec), check_vma=False,
    )
```

profile of v0, /device:TPU:1, one launch (start us, length us, event | category | flops | bytes accessed | tf_op | source)
XLA Modules:
  0.0 78.6 jit_solution(3192132774643231911)
XLA Ops:
  0.6 73.7 %shard_map.85 = f32[3,2,256,256]{3,2,1,0:T(8,128)} custom-call(f32[2,256,256]{2,1,0:T(8,128)} %res_ref.1, f32[2,256,256]{2,1,0:T(8,128)} %dir_ref.1, f32[48,24,128]{2,1,0:T(8,128)} %constant.6.clone.gram_hbm, f32[48,24,128]{2,1,0:T(8,128)} %constant.7.clone.moved_hbm, f32[2,24,128]{2,1,0:T(8,128)} %constant.8.clone.change_tab), custom_call_target="tpu_custom_call" | custom-call | tf_op jit(solution)/shard_map/pallas_call | solution.py:452
  74.4 0.0 copy-start
  74.4 2.3 %slice_bitcast_fusion = (f32[2,256,256]{2,1,0:T(8,128)}, f32[2,256,256]{2,1,0:T(8,128)}) fusion(f32[3,2,256,256]{3,2,1,0:T(8,128)} %shard_map.85), kind=kLoop, calls=%fused_computation.1 | loop fusion | bytes 2097152 | tf_op jit(solution)/shard_map/squeeze | solution.py:476
  76.7 0.0 copy-done
  76.7 1.9 %bitcast_add_fusion = f32[2,256,256]{2,1,0:T(8,128)} fusion(f32[2,256,256]{2,1,0:T(8,128)S(1)} %copy-done, f32[3,2,256,256]{3,2,1,0:T(8,128)} %shard_map.85), kind=kLoop, calls=%fused_computation | loop fusion | flops 131072 | bytes 1572864 | tf_op jit(solution)/shard_map/add | solution.py:476
Async XLA Ops:
  74.4 2.3 %copy-start = (f32[2,256,256]{2,1,0:T(8,128)S(1)}, f32[2,256,256]{2,1,0:T(8,128)}, u32[]{:S(2)}) copy-start(f32[2,256,256]{2,1,0:T(8,128)} %param.6) | copy-start | bytes 1572868
where the time goes:
time: 78.9 us; the launch traced here: 78.6 us
  Pallas kernels  73.7 us (93%)
  local copies, waits for them, and re-layouts  2.32 us (3%)
  other arithmetic  1.9 us (2%)
    pallas_call x1, Pallas kernels, on_device(): pl.pallas_call(functools.partial(kernel, gz_count, ga), out_shape=shape,...  73.7 us
    squeeze x1, local copies, waits for them, and re-layouts, on_device(): return (sol + combined[0], combined[1], combined[2])  2.31 us
    add x1, other arithmetic, on_device(): return (sol + combined[0], combined[1], combined[2])  1.9 us

commit v1 on v0

v1 whole, which is shorter than its diff:
```python
import functools

import jax
import jax.numpy as jnp
import numpy as np
from jax import lax
from jax.experimental import pallas as pl
from jax.experimental.pallas import tpu as pltpu
from jax.sharding import PartitionSpec as P

S = 8
MESH = pl.DeviceIdType.MESH
first_scale = -1.0 / 6.0
next_scale = -1.0 / 3.0
SIDE = 24
LANES = 128
HALVES = S // 2
UNROLL = 4
PIECES = 4
VMEM_LIMIT = 32 * 2 ** 20


def change_matrix(steps):
    count = 2 * steps + 1
    table = np.zeros((count, count), np.float64)
    for offset, length in ((0, steps + 1), (steps + 1, steps)):
        for power in range(length - 1):
            column = offset + power
            table[column, column] = 6.0
            if power == 0:
                table[column + 1, column] = 6.0
            else:
                table[column + 1, column] = 3.0
                table[column - 1, column] = 3.0
    return table


def dd(power, odd):
    return 2 * power + odd


def rr(power, odd):
    return 2 * S + 1 + 2 * power + odd


def dr(power, odd):
    return 4 * S + 2 * power + odd


COUNT = 6 * S


def gram_tables():
    def moment(kind, order):
        half, odd = order // 2, order % 2
        row = np.zeros(COUNT)
        row[kind(half, odd)] += 2.0
        row[kind(0, odd)] -= 1.0
        return row

    size = 2 * S + 1
    table = np.zeros((COUNT, size, size))
    for i in range(size):
        for j in range(size):
            a, b = (i if i <= S else i - S - 1), (j if j <= S else j - S - 1)
            kind = dd if (i <= S and j <= S) else rr if (i > S and j > S) else dr
            table[:, i, j] = 0.5 * (moment(kind, a + b) + moment(kind, abs(a - b)))
    moved = table @ change_matrix(S)

    def padded(t):
        out = np.zeros((t.shape[0], SIDE, LANES), np.float32)
        out[:, :size, :size] = t
        return out

    change = np.stack([change_matrix(S), change_matrix(S).T])
    return padded(table), padded(moved), padded(change)


def flipped(p, bits, group):
    if group & (group - 1):
        return (p + bits) % group
    out, step = p, 1
    while step < group:
        if bits & step:
            out = out + step * (1 - 2 * ((p // step) % 2))
        step *= 2
    return out


def send_order(group):
    if group & (group - 1):
        return list(range(1, group))
    first = [j for j in range(2, group) if (j // 2) & (j // 2 - 1) == 0]
    first = first[::2] + first[1::2]
    return first + [j for j in range(2, group) if j not in first] + [1]


def kernel(gz_count, ga, res_ref, dir_ref, gram_hbm, moved_hbm, change_hbm,
           dx, last, beta_ref,
           X, halo, stage, edge, edge_in, accs, red, coef, out_dx, out_q, held, gram_tab, moved_tab, change_tab,
           in_send, in_recv, own_sem, z_send, z_recv, r_send, r_recv, e_send, e_recv,
           a_send, a_recv, o_send, o_recv, q_send, q_recv, f_send, f_recv, load_sem):
    group = 2 * ga
    groups = gz_count // 2
    count = gz_count * ga
    planes, width, depth = res_ref.shape
    tall = planes * group
    rows = width // group
    iz, ia = lax.axis_index("gz"), lax.axis_index("ga")
    me = iz * ga + ia
    g = iz // 2
    p = (iz % 2) * ga + ia
    order = send_order(group)

    def place(position):
        upper = position // ga
        return upper * (3 * ga - 1 - position) + (1 - upper) * position

    b = place(p)

    def device(which, position):
        return (which * 2 + position // ga, position % ga)

    def block_rows(block):
        return pl.ds(pl.multiple_of(block * rows, rows), rows)

    loads = [pltpu.make_async_copy(source, target, load_sem.at[i]) for i, (source, target) in enumerate((
        (dir_ref, held.at[0]), (res_ref, held.at[1]), (gram_hbm, gram_tab), (moved_hbm, moved_tab),
        (change_hbm, change_tab)))]
    for load in loads:
        load.start()

    below, above = g > 0, g < groups - 1
    before, after = b > 0, b < group - 1
    z_there, r_there = (below, above), (before, after)

    barrier = pltpu.get_barrier_semaphore()

    def greet(target):
        pl.semaphore_signal(barrier, inc=1, device_id=target, device_id_type=MESH)

    if groups - 1 <= HALVES:
        for j in range(1, group):
            greet(device(g, flipped(p, j, group)))
        for up in range(2):
            @pl.when(z_there[up])
            def _():
                greet(device(g + 2 * up - 1, p))
            for side in range(2):
                @pl.when(z_there[up] & r_there[side])
                def _():
                    greet(device(g + 2 * up - 1, place(b + 2 * side - 1)))
        below_1, above_1 = jnp.minimum(g, 1), jnp.minimum(groups - 1 - g, 1)
        before_1, after_1 = jnp.minimum(b, 1), jnp.minimum(group - 1 - b, 1)
        pl.semaphore_wait(barrier, group - 1 + (below_1 + above_1) * (1 + before_1 + after_1))
    else:
        def greet_all(j, carry):
            t = (me + j) % count
            greet((t // ga, t % ga))
            return carry
        lax.fori_loop(1, count, greet_all, 0)
        pl.semaphore_wait(barrier, count - 1)

    def incoming(c, j):
        q = flipped(p, j, group)
        return pltpu.make_async_remote_copy(
            src_ref=held.at[c, :, block_rows(place(q)), :],
            dst_ref=X.at[c, 0, pl.ds(2 + planes * p, planes)],
            send_sem=in_send.at[c, j], recv_sem=in_recv.at[c, j],
            device_id=device(g, q), device_id_type=MESH)

    def incoming_from(c, j):
        return incoming(c, j if group & (group - 1) == 0 else group - j)

    def own_in(c):
        return pltpu.make_async_copy(
            held.at[c, :, block_rows(b), :],
            X.at[c, 0, pl.ds(2 + planes * p, planes)], own_sem.at[c])

    loads[0].wait()
    for j in order:
        incoming(0, j).start()
    own_in(0).start()
    loads[1].wait()
    early = len(order) // 2 + 1
    for j in order[:early]:
        incoming(1, j).start()
    own_in(1).start()

    for side, missing, at in ((0, g == 0, 0), (1, g == groups - 1, tall + 2)):
        @pl.when(missing)
        def _():
            for c in range(2):
                for k in range(0, S, 2):
                    X[c, k, at] = jnp.zeros((rows, depth), jnp.float32)
                    X[c, k, at + 1] = jnp.zeros((rows, depth), jnp.float32)
    for side, missing in ((0, b == 0), (1, b == group - 1)):
        @pl.when(missing)
        def _():
            for c in range(2):
                for k in range(0, S, 2):
                    for d in range(2):
                        halo[c, k, side, d] = jnp.zeros((tall, depth), jnp.float32)
    for up in range(2):
        for side in range(2):
            @pl.when(jnp.logical_not(z_there[up] & r_there[side]))
            def _():
                for c in range(2):
                    for h in range(HALVES):
                        edge_in[c, h, up, side] = jnp.zeros((1, depth), jnp.float32)

    def deep(c, k):
        return 1 if c == 1 and k == S - 2 else 2

    def z_copy(c, k, up):
        d = deep(c, k)
        source = 2 + tall - d if up else 2
        target = 2 - d if up else tall + 2
        return pltpu.make_async_remote_copy(
            src_ref=X.at[c, k, pl.ds(source, d)],
            dst_ref=X.at[c, k, pl.ds(target, d)],
            send_sem=z_send.at[c, k // 2, up], recv_sem=z_recv.at[c, k // 2, up],
            device_id=device(g + 2 * up - 1, p), device_id_type=MESH)

    def r_copy(c, k, up):
        d = deep(c, k)
        return pltpu.make_async_remote_copy(
            src_ref=stage.at[c, k // 2, up, pl.ds(0, d)],
            dst_ref=halo.at[c, k, 1 - up, pl.ds(0, d)],
            send_sem=r_send.at[c, k // 2, up], recv_sem=r_recv.at[c, k // 2, up],
            device_id=device(g, place(b + 2 * up - 1)), device_id_type=MESH)

    def e_copy(c, k, up, side):
        return pltpu.make_async_remote_copy(
            src_ref=edge.at[c, k // 2, up, side],
            dst_ref=edge_in.at[c, k // 2, 1 - up, 1 - side],
            send_sem=e_send.at[c, k // 2, up, side], recv_sem=e_recv.at[c, k // 2, 1 - up, 1 - side],
            device_id=device(g + 2 * up - 1, place(b + 2 * side - 1)), device_id_type=MESH)

    def e_arrival(c, k, up, side):
        return pltpu.make_async_remote_copy(
            src_ref=edge.at[c, k // 2, up, side],
            dst_ref=edge_in.at[c, k // 2, up, side],
            send_sem=e_send.at[c, k // 2, up, side], recv_sem=e_recv.at[c, k // 2, up, side],
            device_id=device(g + 2 * up - 1, place(b + 2 * side - 1)), device_id_type=MESH)

    def send_z(c, k):
        for up in range(2):
            @pl.when(z_there[up])
            def _():
                z_copy(c, k, up).start()

    def send_edges(c, k):
        for up in range(2):
            for side in range(2):
                edge[c, k // 2, up, side] = X[c, k, 2 + (tall - 1) * up, (rows - 1) * side:(rows - 1) * side + 1, :]
        for up in range(2):
            for side in range(2):
                @pl.when(z_there[up] & r_there[side])
                def _():
                    e_copy(c, k, up, side).start()

    def send_rows(c, k):
        for side in range(2):
            @pl.when(r_there[side])
            def _():
                r_copy(c, k, side).start()

    def receive(c, k):
        for side in range(2):
            @pl.when(r_there[side])
            def _():
                r_copy(c, k, 1 - side).wait_recv()
        for up in range(2):
            if deep(c, k) == 2:
                for side in range(2):
                    @pl.when(z_there[up] & r_there[side])
                    def _():
                        e_arrival(c, k, up, side).wait_recv()

            @pl.when(z_there[up])
            def _():
                z_copy(c, k, 1 - up).wait_recv()

    def iotas(height):
        row_ids = lax.broadcasted_iota(jnp.int32, (height, depth), 0)
        col_ids = lax.broadcasted_iota(jnp.int32, (height, depth), 1)
        return row_ids == 0, row_ids == height - 1, col_ids == 0, col_ids == depth - 1

    def folded(x):
        total = x[0:8]
        for i in range(8, rows, 8):
            total = total + x[i:i + 8]
        out = total[:, 0:LANES]
        for i in range(LANES, depth, LANES):
            out = out + total[:, i:i + LANES]
        return out

    def neighbours(cur, total, low, high, masks):
        height = cur.shape[0]
        first_row, last_row, first_col, last_col = masks
        total = total + jnp.where(first_row, low, pltpu.roll(cur, 1, 0))
        total = total + jnp.where(last_row, high, pltpu.roll(cur, height - 1, 0))
        total = total + jnp.where(first_col, 0.0, pltpu.roll(cur, 1, 1))
        return total + jnp.where(last_col, 0.0, pltpu.roll(cur, depth - 1, 1))

    plane_masks, row_masks = iotas(rows), iotas(tall)
    z_scale = [jnp.minimum(g, 1).astype(jnp.float32), jnp.minimum(groups - 1 - g, 1).astype(jnp.float32)]
    r_scale = [jnp.minimum(b, 1).astype(jnp.float32), jnp.minimum(group - 1 - b, 1).astype(jnp.float32)]

    def extend(c, k):
        scale = first_scale if k == 1 else next_scale
        h = (k - 1) // 2
        for side in range(2):
            cur = halo[c, k - 1, side, 0]
            total = halo[c, k - 1, side, 1] + stage[c, h, side, 0]
            total = neighbours(cur, total, edge_in[c, h, 0, side], edge_in[c, h, 1, side], row_masks)
            new = total * (r_scale[side] * scale)
            if k > 1:
                new = new - halo[c, k - 2, side, 0]
            halo[c, k, side, 0] = new
        for up in range(2):
            at, out, inside = (tall + 2, tall + 3, tall + 1) if up else (1, 0, 2)
            cur = X[c, k - 1, at]
            total = X[c, k - 1, out] + X[c, k - 1, inside]
            total = neighbours(cur, total, edge_in[c, h, up, 0], edge_in[c, h, up, 1], plane_masks)
            new = total * (z_scale[up] * scale)
            if k > 1:
                new = new - X[c, k - 2, at]
            X[c, k, at] = new

    def names_of(c, k):
        if c == 0:
            names = [(dd(k, 0), "new", "new"), (dd(k - 1, 1), "new", "cur")]
            if k == 1:
                names.append((dd(0, 0), "cur", "cur"))
        else:
            names = [(rr(k, 0), "new", "new"), (rr(k - 1, 1), "new", "cur"),
                     (dr(k, 0), "new", "other"), (dr(k - 1, 1), "cur", "other")]
            if k == S - 1:
                names.append((dr(k, 1), "new", "ahead"))
            if k == 1:
                names += [(rr(0, 0), "cur", "cur"), (dr(0, 0), "cur", "start")]
        return names

    def sent(c, k):
        return k % 2 == 0 and k < (S if c == 0 else S - 1)

    def plane(c, k, z, sums):
        names = names_of(c, k)
        cur = X[c, k - 1, z + 2]
        total = X[c, k - 1, z + 1] + X[c, k - 1, z + 3]
        low = halo[c, k - 1, 0, 0, pl.ds(z, 1), :]
        high = halo[c, k - 1, 1, 0, pl.ds(z, 1), :]
        total = neighbours(cur, total, low, high, plane_masks)
        if k == 1:
            new = total * first_scale
        else:
            new = total * next_scale - X[c, k - 2, z + 2]
        X[c, k, z + 2] = new
        if sent(c, k):
            put_rows(c, k, z, new)
        have = {"new": new, "cur": cur}
        if any("other" in n for n in names):
            have["other"] = X[0, k, z + 2]
        if any("ahead" in n for n in names):
            have["ahead"] = X[0, k + 1, z + 2]
        if any("start" in n for n in names):
            have["start"] = X[0, 0, z + 2]
        return tuple(s + folded(have[l] * have[r]) for s, (_, l, r) in zip(sums, names))

    def put_rows(c, k, z, new):
        at = pl.ds(z, 1)
        stage[c, k // 2, 0, 0, at, :] = new[0:1]
        stage[c, k // 2, 1, 0, at, :] = new[rows - 1:rows]
        if deep(c, k) == 2:
            stage[c, k // 2, 0, 1, at, :] = new[1:2]
            stage[c, k // 2, 1, 1, at, :] = new[rows - 2:rows - 1]

    def zero_sums(c, k):
        return tuple(jnp.zeros((8, LANES), jnp.float32) for _ in names_of(c, k))

    def keep(c, k, sums):
        for s, (slot, _, _) in zip(sums, names_of(c, k)):
            accs[slot] = s

    def ends(c, k, width_of, sums):
        def body(i, sums):
            return plane(c, k, i + (i // width_of) * (tall - 2 * width_of), sums)
        return lax.fori_loop(0, 2 * width_of, body, sums, unroll=True)

    def middle(c, k, width_of, sums):
        length = tall - 2 * width_of
        unroll = max(u for u in range(1, UNROLL + 1) if length % u == 0)
        return lax.fori_loop(width_of, tall - width_of, lambda z, s: plane(c, k, z, s), sums, unroll=unroll)

    def chain_round(c, k):
        a = k + 1
        top = S if c == 0 else S - 1
        if a == top:
            keep(c, a, middle(c, a, 0, zero_sums(c, a)))
            return
        n = k + 2
        extend(c, a)
        sums = ends(c, a, 3, zero_sums(c, a))
        later = ends(c, n, 2, zero_sums(c, n))
        if sent(c, n):
            send_z(c, n)
            if deep(c, n) == 2:
                send_edges(c, n)
        keep(c, a, middle(c, a, 3, sums))
        later = middle(c, n, 2, later)
        if sent(c, n):
            send_rows(c, n)
        keep(c, n, later)

    def arrive(c):
        own_in(c).wait()
        for j in order:
            incoming_from(c, j).wait_recv()
        send_z(c, 0)
        send_edges(c, 0)

        def copy_rows(z, carry):
            put_rows(c, 0, z, X[c, 0, z + 2])
            return carry
        lax.fori_loop(0, tall, copy_rows, 0, unroll=4)
        send_rows(c, 0)

    arrive(0)
    for j in order[early:]:
        incoming(1, j).start()
    receive(0, 0)
    chain_round(0, 0)
    arrive(1)
    for k in range(0, S, 2):
        if k:
            receive(0, k)
            chain_round(0, k)
        receive(1, k)
        chain_round(1, k)

    lanes = lax.broadcasted_iota(jnp.int32, (8, LANES), 1)
    packed = jnp.zeros((8, LANES), jnp.float32)
    for t in range(COUNT // 8):
        part = jnp.sum(jnp.sum(accs[8 * t:8 * t + 8], axis=1), axis=1, keepdims=True)
        packed = packed + jnp.where(lanes == t, part, 0.0)
    red[me] = jnp.sum(pltpu.roll(packed, 0, 1, stride=8, stride_axis=0), axis=0, keepdims=True)

    def moments_to(j):
        t = (me + j) % count
        return pltpu.make_async_remote_copy(
            src_ref=red.at[me], dst_ref=red.at[me], send_sem=a_send.at[0], recv_sem=a_recv.at[0],
            device_id=(t // ga, t % ga), device_id_type=MESH)

    def start_moments(j, carry):
        moments_to(j).start()
        return carry

    lax.fori_loop(1, count, start_moments, 0)
    others = red.at[pl.ds(0, count - 1)]
    pltpu.make_async_copy(others, others, a_recv.at[0]).wait()
    total = jnp.sum(red[...], axis=0)

    loads[2].wait()
    loads[3].wait()
    loads[4].wait()
    gram = jnp.zeros((SIDE, LANES), jnp.float32)
    moved = jnp.zeros((SIDE, LANES), jnp.float32)
    for e in range(COUNT):
        at = 8 * (e % 8) + e // 8
        value = total[0:1, at:at + 1]
        gram = gram + value * gram_tab[e]
        moved = moved + value * moved_tab[e]
    change, change_t = change_tab[0], change_tab[1]

    def full(x):
        return jnp.sum(jnp.sum(x, axis=0, keepdims=True), axis=1, keepdims=True)

    def unit(axis, at):
        ids = lax.broadcasted_iota(jnp.int32, (SIDE, LANES), axis)
        return jnp.where(ids == at, 1.0, 0.0).astype(jnp.float32)

    def advance(state):
        qc, qr, wc, wr, it, rho = state
        alpha = rho / full(qc * (moved * qr))
        mc = jnp.sum(change * qr, axis=1, keepdims=True)
        mr = jnp.sum(change_t * qc, axis=0, keepdims=True)
        it = it + alpha * qc
        wc = wc - alpha * mc
        wr = wr - alpha * mr
        rho_new = full(wc * (gram * wr))
        return wc, wr, it, rho_new, rho_new / rho

    def inner(_, state):
        wc, wr, it, rho, beta = advance(state)
        return wc + beta * state[0], wr + beta * state[1], wc, wr, it, rho

    wc, wr = unit(0, S + 1), unit(1, S + 1)
    state = (unit(0, 0), unit(1, 0), wc, wr, jnp.zeros((SIDE, LANES), jnp.float32),
             full(wc * (gram * wr)))
    state = lax.fori_loop(0, S - 1, inner, state)
    _, _, it, _, beta = advance(state)
    coef[0] = it
    coef[1] = state[0]
    beta_ref[...] = jnp.zeros((8, LANES), jnp.float32) + beta

    def combine(q):
        start = planes * q + 1 + q % 2

        def strip(s, carry):
            i, part = s // (rows // 8), s % (rows // 8)
            at = pl.ds(pl.multiple_of(part * 8, 8), 8)
            sums = [None, None]
            for v in range(2 * S - 1):
                c, k = (0, v) if v < S else (1, v - S)
                row = v if v < S else v + 1
                x = X[c, k, start + i, at, :]
                for o in range(2):
                    f = coef[o, row:row + 1, :]
                    f = jnp.concatenate([f] * (depth // LANES), axis=1)
                    term = f * x
                    sums[o] = term if sums[o] is None else sums[o] + term
            out_dx[q, i, at, :] = sums[0]
            out_q[q, i, at, :] = sums[1]
            return carry
        lax.fori_loop(0, (planes + 1) * (rows // 8), strip, 0, unroll=2)

    odd = p % 2

    def outgoing_dx(j):
        q = flipped(p, j, group)
        return pltpu.make_async_remote_copy(
            src_ref=out_dx.at[q], dst_ref=dx.at[pl.ds(q % 2, planes + 1), block_rows(b), :],
            send_sem=o_send.at[j], recv_sem=o_recv.at[j],
            device_id=device(g, q), device_id_type=MESH)

    def outgoing_q(j):
        q = flipped(p, j, group)
        return pltpu.make_async_remote_copy(
            src_ref=out_q.at[q, pl.ds(1 - q % 2, planes)], dst_ref=last.at[:, block_rows(b), :],
            send_sem=q_send.at[j], recv_sem=q_recv.at[j],
            device_id=device(g, q), device_id_type=MESH)

    def source_of(j):
        return flipped(p, j, group) if group & (group - 1) == 0 else (p + group - j) % group

    def dx_from(j):
        at = block_rows(place(source_of(j)))
        return pltpu.make_async_remote_copy(
            src_ref=out_dx.at[p], dst_ref=dx.at[pl.ds(odd, planes + 1), at, :],
            send_sem=o_send.at[j], recv_sem=o_recv.at[j],
            device_id=device(g, source_of(j)), device_id_type=MESH)

    def q_from(j):
        at = block_rows(place(source_of(j)))
        return pltpu.make_async_remote_copy(
            src_ref=out_q.at[p, pl.ds(1 - odd, planes)], dst_ref=last.at[:, at, :],
            send_sem=q_send.at[j], recv_sem=q_recv.at[j],
            device_id=device(g, source_of(j)), device_id_type=MESH)

    mate = p + 1 - 2 * odd

    def forwarded(block):
        at = block_rows(block)
        return pltpu.make_async_remote_copy(
            src_ref=dx.at[planes - odd * (planes - 1), at, :],
            dst_ref=dx.at[(1 - odd) * (planes + 1), at, :],
            send_sem=f_send.at[block], recv_sem=f_recv.at[block],
            device_id=device(g, mate), device_id_type=MESH)

    def forward_of(block):
        at = block_rows(block)
        return pltpu.make_async_remote_copy(
            src_ref=dx.at[planes - odd * (planes - 1), at, :],
            dst_ref=dx.at[odd * (planes + 1), at, :],
            send_sem=f_send.at[block], recv_sem=f_recv.at[block],
            device_id=device(g, mate), device_id_type=MESH)

    for j in order:
        combine(flipped(p, j, group))
        outgoing_dx(j).start()
    combine(p)
    for j in order:
        outgoing_q(j).start()
    own = pltpu.make_async_copy(out_dx.at[p], dx.at[pl.ds(odd, planes + 1), block_rows(b), :], own_sem.at[2])
    own.start()
    own_q = pltpu.make_async_copy(out_q.at[p, pl.ds(1 - odd, planes)], last.at[:, block_rows(b), :], own_sem.at[3])
    own_q.start()
    own.wait()
    forward_of(b).start()
    for j in [order[-1]] + order[:-1]:
        dx_from(j).wait_recv()
        forward_of(place(source_of(j))).start()
    own_q.wait()
    for block in range(group):
        forwarded(block).wait_recv()
    for j in order:
        q_from(j).wait_recv()

    for c in range(2):
        for j in order:
            incoming(c, j).wait_send()
        for k in range(0, S, 2):
            for up in range(2):
                @pl.when(z_there[up])
                def _():
                    z_copy(c, k, up).wait_send()

                @pl.when(r_there[up])
                def _():
                    r_copy(c, k, up).wait_send()

                if deep(c, k) == 2:
                    for side in range(2):
                        @pl.when(z_there[up] & r_there[side])
                        def _():
                            e_copy(c, k, up, side).wait_send()
    pltpu.make_async_copy(others, others, a_send.at[0]).wait()
    for j in order:
        outgoing_dx(j).wait_send()
        outgoing_q(j).wait_send()
    for block in range(group):
        forward_of(block).wait_send()


def finish(sol, res, dx, last, beta, sol_out, res_out, dir_out, buf, sem):
    planes, width, depth = sol.shape
    piece = width // PIECES
    row_ids = lax.broadcasted_iota(jnp.int32, (piece, depth), 0)
    col_ids = lax.broadcasted_iota(jnp.int32, (piece, depth), 1)
    factor = jnp.concatenate([beta[0:1, :]] * (depth // LANES), axis=1)
    copies = []
    for i in range(planes):
        for s in range(PIECES):
            at = pl.ds(s * piece, piece)
            cur = dx[i + 1, at, :]
            low = dx[i + 1, s * piece - 1:s * piece, :] if s else jnp.zeros((1, depth), jnp.float32)
            high = dx[i + 1, (s + 1) * piece:(s + 1) * piece + 1, :] if s < PIECES - 1 else jnp.zeros((1, depth), jnp.float32)
            total = dx[i, at, :] + dx[i + 2, at, :]
            total = total + jnp.where(row_ids == 0, low, pltpu.roll(cur, 1, 0))
            total = total + jnp.where(row_ids == piece - 1, high, pltpu.roll(cur, piece - 1, 0))
            total = total + jnp.where(col_ids == 0, 0.0, pltpu.roll(cur, 1, 1))
            total = total + jnp.where(col_ids == depth - 1, 0.0, pltpu.roll(cur, depth - 1, 1))
            buf[0, i, at, :] = sol[i, at, :] + cur
            remain = res[i, at, :] - (6.0 * cur - total)
            buf[1, i, at, :] = remain
            buf[2, i, at, :] = remain + factor * last[i, at, :]
            for o, target in enumerate((sol_out, res_out, dir_out)):
                copy = pltpu.make_async_copy(buf.at[o, i, at, :], target.at[i, at, :], sem.at[o, i, s])
                copy.start()
                copies.append(copy)
    for copy in copies:
        copy.wait()


def on_device(gz_count, ga, sol, res, direction):
    planes, width, depth = sol.shape
    group, groups = 2 * ga, gz_count // 2
    tall, rows = planes * group, width // group
    gram_tab, moved_tab, change_tab = (jnp.asarray(t) for t in gram_tables())
    vmem = pl.BlockSpec(memory_space=pltpu.VMEM)
    dma = pltpu.SemaphoreType.DMA
    anywhere = pl.BlockSpec(memory_space=pltpu.HBM)
    f32 = jnp.float32
    dx, last, beta = pl.pallas_call(
        functools.partial(kernel, gz_count, ga),
        out_shape=[pltpu.VMEM((planes + 2, width, depth), f32), pltpu.VMEM((planes, width, depth), f32),
                   pltpu.VMEM((8, LANES), f32)],
        in_specs=[anywhere] * 5,
        out_specs=[vmem] * 3,
        scratch_shapes=[
            pltpu.VMEM((2, S + 1, tall + 4, rows, depth), f32),
            pltpu.VMEM((2, S, 2, 2, tall, depth), f32),
            pltpu.VMEM((2, HALVES, 2, 2, tall, depth), f32),
            pltpu.VMEM((2, HALVES, 2, 2, 1, depth), f32),
            pltpu.VMEM((2, HALVES, 2, 2, 1, depth), f32),
            pltpu.VMEM((COUNT, 8, LANES), f32),
            pltpu.VMEM((gz_count * ga, 1, LANES), f32),
            pltpu.VMEM((2, SIDE, LANES), f32),
            pltpu.VMEM((group, planes + 1, rows, depth), f32),
            pltpu.VMEM((group, planes + 1, rows, depth), f32),
            pltpu.VMEM((2, planes, width, depth), f32),
            pltpu.VMEM((COUNT, SIDE, LANES), f32),
            pltpu.VMEM((COUNT, SIDE, LANES), f32),
            pltpu.VMEM((2, SIDE, LANES), f32),
            dma((2, group)), dma((2, group)), dma((4,)),
            dma((2, HALVES, 2)), dma((2, HALVES, 2)), dma((2, HALVES, 2)), dma((2, HALVES, 2)),
            dma((2, HALVES, 2, 2)), dma((2, HALVES, 2, 2)),
            dma((1,)), dma((1,)),
            dma((group,)), dma((group,)), dma((group,)), dma((group,)), dma((group,)), dma((group,)),
            dma((5,)),
        ],
        compiler_params=pltpu.CompilerParams(collective_id=0, has_side_effects=True, vmem_limit_bytes=VMEM_LIMIT),
    )(*(pltpu.with_memory_space_constraint(x, pltpu.HBM) for x in (res, direction, gram_tab, moved_tab, change_tab)))
    shape = jax.ShapeDtypeStruct(sol.shape, f32)
    return pl.pallas_call(
        finish,
        out_shape=[shape] * 3,
        in_specs=[vmem] * 5,
        out_specs=[anywhere] * 3,
        scratch_shapes=[pltpu.VMEM((3,) + sol.shape, f32), dma((3, planes, PIECES))],
        compiler_params=pltpu.CompilerParams(vmem_limit_bytes=8 * 2 ** 20),
    )(sol, res, dx, last, beta)


def solution(mesh):
    spec = P(("gz", "ga"), None, None)
    return jax.shard_map(
        functools.partial(on_device, mesh.shape["gz"], mesh.shape["ga"]),
        mesh=mesh, in_specs=(spec, spec, spec), out_specs=(spec, spec, spec), check_vma=False,
    )
```

time: 78.9 us -> 62.1 us (0.79)
  Pallas kernels: 73.7 us -> 61.3 us
  local copies, waits for them, and re-layouts: 2.32 us -> 0.01 us
  other arithmetic: 1.9 us -> 0 us
    pallas_call x1 -> x2, Pallas kernels: 73.7 us -> 61.3 us  [the longest x1 59.9 us: on_device(): pl.pallas_call(functools.partial(kernel, gz_count, ga), out_shape=[pltpu....]
    squeeze x1 -> x0, local copies, waits for them, and re-layouts: 2.31 us -> none  [on_device(): return (sol + combined[0], combined[1], combined[2])]
    add x1 -> x0, other arithmetic: 1.9 us -> none  [on_device(): return (sol + combined[0], combined[1], combined[2])]
where the time goes in v1:
time: 62.1 us; the launch traced here: 62 us
  Pallas kernels  61.3 us (99%)
  between operations  0.67 us (1%)
    pallas_call x1, Pallas kernels, on_device(): pl.pallas_call(functools.partial(kernel, gz_count, ga), out_shape=[pltpu....  59.9 us
    pallas_call x1, Pallas kernels, on_device(): pl.pallas_call(finish, out_shape=[shape] * 3, in_specs=[vmem] * 5, out_sp...  1.45 us

profile of v1, /device:TPU:1, one launch (start us, length us, event | category | flops | bytes accessed | tf_op | source)
XLA Modules:
  0.0 62.0 jit_solution(1013699685111975340)
XLA Ops:
  0.6 0.0 copy-start
  0.6 0.0 copy-start.1
  0.7 59.9 %shard_map.85 = (f32[4,256,256]{2,1,0:T(8,128)S(1)}, f32[2,256,256]{2,1,0:T(8,128)S(1)}, f32[8,128]{1,0:T(8,128)S(1)}) custom-call(f32[2,256,256]{2,1,0:T(8,128)} %res.1, f32[2,256,256]{2,1,0:T(8,128)} %dir_ref.1, f32[48,24,128]{2,1,0:T(8,128)} %constant.6.clone.gram_hbm, f32[48,24,128]{2,1,0:T(8,128)} %constant.7.clone.moved_hbm, ...), custom_call_target="tpu_custom_call" | custom-call | tf_op jit(solution)/shard_map/pallas_call | solution.py:666
  60.5 0.0 copy-done
  60.5 0.0 copy-done.1
  60.5 1.5 %shard_map.86 = (f32[2,256,256]{2,1,0:T(8,128)}, f32[2,256,256]{2,1,0:T(8,128)}, f32[2,256,256]{2,1,0:T(8,128)}) custom-call(f32[2,256,256]{2,1,0:T(8,128)S(1)} %copy-done.1, f32[2,256,256]{2,1,0:T(8,128)S(1)} %copy-done, f32[4,256,256]{2,1,0:T(8,128)S(1)} %get-tuple-element.6.dx, f32[2,256,256]{2,1,0:T(8,128)S(1)} %get-tuple-element.7.last, ...), custom_call_target="tpu_custom_call" | custom-call | tf_op jit(solution)/shard_map/pallas_call | solution.py:697
Async XLA Ops:
  0.6 59.9 %copy-start = (f32[2,256,256]{2,1,0:T(8,128)S(1)}, f32[2,256,256]{2,1,0:T(8,128)}, u32[]{:S(2)}) copy-start(f32[2,256,256]{2,1,0:T(8,128)} %res.1) | copy-start | bytes 1572868
  0.6 59.9 %copy-start.1 = (f32[2,256,256]{2,1,0:T(8,128)S(1)}, f32[2,256,256]{2,1,0:T(8,128)}, u32[]{:S(2)}) copy-start(f32[2,256,256]{2,1,0:T(8,128)} %sol.1) | copy-start | bytes 1572868

commit v2 on v1

--- a/solution.py
+++ b/solution.py
@@ -15,7 +15,7 @@
 SIDE = 24
 LANES = 128
 HALVES = S // 2
-UNROLL = 4
+UNROLL = 12
 PIECES = 4
 VMEM_LIMIT = 32 * 2 ** 20
 
@@ -95,9 +95,9 @@
     return first + [j for j in range(2, group) if j not in first] + [1]
 
 
-def kernel(gz_count, ga, res_ref, dir_ref, gram_hbm, moved_hbm, change_hbm,
+def kernel(gz_count, ga, res_ref, dir_ref, table_hbm,
            dx, last, beta_ref,
-           X, halo, stage, edge, edge_in, accs, red, coef, out_dx, out_q, held, gram_tab, moved_tab, change_tab,
+           X, halo, stage, edge, edge_in, accs, red, coef, out_dx, out_q, held, table,
            in_send, in_recv, own_sem, z_send, z_recv, r_send, r_recv, e_send, e_recv,
            a_send, a_recv, o_send, o_recv, q_send, q_recv, f_send, f_recv, load_sem):
     group = 2 * ga
@@ -125,8 +125,7 @@
         return pl.ds(pl.multiple_of(block * rows, rows), rows)
 
     loads = [pltpu.make_async_copy(source, target, load_sem.at[i]) for i, (source, target) in enumerate((
-        (dir_ref, held.at[0]), (res_ref, held.at[1]), (gram_hbm, gram_tab), (moved_hbm, moved_tab),
-        (change_hbm, change_tab)))]
+        (dir_ref, held.at[0]), (res_ref, held.at[1]), (table_hbm, table)))]
     for load in loads:
         load.start()
 
@@ -166,11 +165,8 @@
         return pltpu.make_async_remote_copy(
             src_ref=held.at[c, :, block_rows(place(q)), :],
             dst_ref=X.at[c, 0, pl.ds(2 + planes * p, planes)],
-            send_sem=in_send.at[c, j], recv_sem=in_recv.at[c, j],
+            send_sem=in_send.at[0], recv_sem=in_recv.at[c],
             device_id=device(g, q), device_id_type=MESH)
-
-    def incoming_from(c, j):
-        return incoming(c, j if group & (group - 1) == 0 else group - j)
 
     def own_in(c):
         return pltpu.make_async_copy(
@@ -219,29 +215,28 @@
         return pltpu.make_async_remote_copy(
             src_ref=X.at[c, k, pl.ds(source, d)],
             dst_ref=X.at[c, k, pl.ds(target, d)],
-            send_sem=z_send.at[c, k // 2, up], recv_sem=z_recv.at[c, k // 2, up],
+            send_sem=z_send.at[up], recv_sem=z_recv.at[c, k // 2 % 2, up],
             device_id=device(g + 2 * up - 1, p), device_id_type=MESH)
 
     def r_copy(c, k, up):
-        d = deep(c, k)
-        return pltpu.make_async_remote_copy(
-            src_ref=stage.at[c, k // 2, up, pl.ds(0, d)],
-            dst_ref=halo.at[c, k, 1 - up, pl.ds(0, d)],
-            send_sem=r_send.at[c, k // 2, up], recv_sem=r_recv.at[c, k // 2, up],
+        return pltpu.make_async_remote_copy(
+            src_ref=stage.at[c, k // 2, up],
+            dst_ref=halo.at[c, k, 1 - up],
+            send_sem=r_send.at[up], recv_sem=r_recv.at[c, k // 2 % 2, up],
             device_id=device(g, place(b + 2 * up - 1)), device_id_type=MESH)
 
     def e_copy(c, k, up, side):
         return pltpu.make_async_remote_copy(
             src_ref=edge.at[c, k // 2, up, side],
             dst_ref=edge_in.at[c, k // 2, 1 - up, 1 - side],
-            send_sem=e_send.at[c, k // 2, up, side], recv_sem=e_recv.at[c, k // 2, 1 - up, 1 - side],
+            send_sem=e_send.at[up, side], recv_sem=e_recv.at[c, k // 2 % 2, 1 - up, 1 - side],
             device_id=device(g + 2 * up - 1, place(b + 2 * side - 1)), device_id_type=MESH)
 
     def e_arrival(c, k, up, side):
         return pltpu.make_async_remote_copy(
             src_ref=edge.at[c, k // 2, up, side],
             dst_ref=edge_in.at[c, k // 2, up, side],
-            send_sem=e_send.at[c, k // 2, up, side], recv_sem=e_recv.at[c, k // 2, up, side],
+            send_sem=e_send.at[up, side], recv_sem=e_recv.at[c, k // 2 % 2, up, side],
             device_id=device(g + 2 * up - 1, place(b + 2 * side - 1)), device_id_type=MESH)
 
     def send_z(c, k):
@@ -272,11 +267,10 @@
             def _():
                 r_copy(c, k, 1 - side).wait_recv()
         for up in range(2):
-            if deep(c, k) == 2:
-                for side in range(2):
-                    @pl.when(z_there[up] & r_there[side])
-                    def _():
-                        e_arrival(c, k, up, side).wait_recv()
+            for side in range(2):
+                @pl.when(z_there[up] & r_there[side])
+                def _():
+                    e_arrival(c, k, up, side).wait_recv()
 
             @pl.when(z_there[up])
             def _():
@@ -373,9 +367,8 @@
         at = pl.ds(z, 1)
         stage[c, k // 2, 0, 0, at, :] = new[0:1]
         stage[c, k // 2, 1, 0, at, :] = new[rows - 1:rows]
-        if deep(c, k) == 2:
-            stage[c, k // 2, 0, 1, at, :] = new[1:2]
-            stage[c, k // 2, 1, 1, at, :] = new[rows - 2:rows - 1]
+        stage[c, k // 2, 0, 1, at, :] = new[1:2]
+        stage[c, k // 2, 1, 1, at, :] = new[rows - 2:rows - 1]
 
     def zero_sums(c, k):
         return tuple(jnp.zeros((8, LANES), jnp.float32) for _ in names_of(c, k))
@@ -406,8 +399,7 @@
         later = ends(c, n, 2, zero_sums(c, n))
         if sent(c, n):
             send_z(c, n)
-            if deep(c, n) == 2:
-                send_edges(c, n)
+            send_edges(c, n)
         keep(c, a, middle(c, a, 3, sums))
         later = middle(c, n, 2, later)
         if sent(c, n):
@@ -416,8 +408,8 @@
 
     def arrive(c):
         own_in(c).wait()
-        for j in order:
-            incoming_from(c, j).wait_recv()
+        others = held.at[c, :, pl.ds(0, width - rows), :]
+        pltpu.make_async_copy(others, others, in_recv.at[c]).wait()
         send_z(c, 0)
         send_edges(c, 0)
 
@@ -457,50 +449,70 @@
         moments_to(j).start()
         return carry
 
-    lax.fori_loop(1, count, start_moments, 0)
+    lax.fori_loop(1, count, start_moments, 0, unroll=count <= 64)
+    def drained(ref, sem):
+        pltpu.make_async_copy(ref, ref, sem).wait()
+
+    drained(held.at[:, :, pl.ds(0, width - rows), :], in_send.at[0])
+    for up in range(2):
+        @pl.when(z_there[up])
+        def _():
+            drained(X.at[0, pl.ds(0, S // 2 + 1), pl.ds(0, 3)], z_send.at[up])
+
+        @pl.when(r_there[up])
+        def _():
+            drained(stage.at[:, :, 0], r_send.at[up])
+
+        for side in range(2):
+            @pl.when(z_there[up] & r_there[side])
+            def _():
+                drained(edge.at[:, :, 0, 0], e_send.at[up, side])
     others = red.at[pl.ds(0, count - 1)]
-    pltpu.make_async_copy(others, others, a_recv.at[0]).wait()
+    drained(others, a_recv.at[0])
     total = jnp.sum(red[...], axis=0)
 
     loads[2].wait()
-    loads[3].wait()
-    loads[4].wait()
     gram = jnp.zeros((SIDE, LANES), jnp.float32)
     moved = jnp.zeros((SIDE, LANES), jnp.float32)
     for e in range(COUNT):
         at = 8 * (e % 8) + e // 8
         value = total[0:1, at:at + 1]
-        gram = gram + value * gram_tab[e]
-        moved = moved + value * moved_tab[e]
-    change, change_t = change_tab[0], change_tab[1]
-
-    def full(x):
-        return jnp.sum(jnp.sum(x, axis=0, keepdims=True), axis=1, keepdims=True)
+        gram = gram + value * table[e]
+        moved = moved + value * table[COUNT + e]
+    change, change_t = table[2 * COUNT], table[2 * COUNT + 1]
 
     def unit(axis, at):
         ids = lax.broadcasted_iota(jnp.int32, (SIDE, LANES), axis)
         return jnp.where(ids == at, 1.0, 0.0).astype(jnp.float32)
 
+    def down(x):
+        return jnp.sum(x, axis=0, keepdims=True)
+
+    def across(x):
+        return jnp.sum(x, axis=1, keepdims=True)
+
     def advance(state):
-        qc, qr, wc, wr, it, rho = state
-        alpha = rho / full(qc * (moved * qr))
-        mc = jnp.sum(change * qr, axis=1, keepdims=True)
-        mr = jnp.sum(change_t * qc, axis=0, keepdims=True)
+        qc, qr, wc, wr, it, uc, rho = state
+        mc = across(change * qr)
+        gc = across(moved * qr)
+        mr = down(change_t * qc)
+        alpha = rho / down(qc * gc)
         it = it + alpha * qc
         wc = wc - alpha * mc
         wr = wr - alpha * mr
-        rho_new = full(wc * (gram * wr))
-        return wc, wr, it, rho_new, rho_new / rho
+        uc = uc - alpha * gc
+        rho_new = down(wc * uc)
+        return wc, wr, it, uc, rho_new, rho_new / rho
 
     def inner(_, state):
-        wc, wr, it, rho, beta = advance(state)
-        return wc + beta * state[0], wr + beta * state[1], wc, wr, it, rho
+        wc, wr, it, uc, rho, beta = advance(state)
+        return wc + beta * state[0], wr + beta * state[1], wc, wr, it, uc, rho
 
     wc, wr = unit(0, S + 1), unit(1, S + 1)
-    state = (unit(0, 0), unit(1, 0), wc, wr, jnp.zeros((SIDE, LANES), jnp.float32),
-             full(wc * (gram * wr)))
+    start = across(gram * wr) + jnp.zeros((SIDE, LANES), jnp.float32)
+    state = (unit(0, 0), unit(1, 0), wc, wr, jnp.zeros((SIDE, LANES), jnp.float32), start, down(wc * start))
     state = lax.fori_loop(0, S - 1, inner, state)
-    _, _, it, _, beta = advance(state)
+    _, _, it, _, _, beta = advance(state)
     coef[0] = it
     coef[1] = state[0]
     beta_ref[...] = jnp.zeros((8, LANES), jnp.float32) + beta
@@ -532,14 +544,14 @@
         q = flipped(p, j, group)
         return pltpu.make_async_remote_copy(
             src_ref=out_dx.at[q], dst_ref=dx.at[pl.ds(q % 2, planes + 1), block_rows(b), :],
-            send_sem=o_send.at[j], recv_sem=o_recv.at[j],
+            send_sem=o_send.at[0], recv_sem=o_recv.at[j],
             device_id=device(g, q), device_id_type=MESH)
 
     def outgoing_q(j):
         q = flipped(p, j, group)
         return pltpu.make_async_remote_copy(
             src_ref=out_q.at[q, pl.ds(1 - q % 2, planes)], dst_ref=last.at[:, block_rows(b), :],
-            send_sem=q_send.at[j], recv_sem=q_recv.at[j],
+            send_sem=q_send.at[0], recv_sem=q_recv.at[0],
             device_id=device(g, q), device_id_type=MESH)
 
     def source_of(j):
@@ -549,32 +561,17 @@
         at = block_rows(place(source_of(j)))
         return pltpu.make_async_remote_copy(
             src_ref=out_dx.at[p], dst_ref=dx.at[pl.ds(odd, planes + 1), at, :],
-            send_sem=o_send.at[j], recv_sem=o_recv.at[j],
+            send_sem=o_send.at[0], recv_sem=o_recv.at[j],
             device_id=device(g, source_of(j)), device_id_type=MESH)
 
-    def q_from(j):
-        at = block_rows(place(source_of(j)))
-        return pltpu.make_async_remote_copy(
-            src_ref=out_q.at[p, pl.ds(1 - odd, planes)], dst_ref=last.at[:, at, :],
-            send_sem=q_send.at[j], recv_sem=q_recv.at[j],
-            device_id=device(g, source_of(j)), device_id_type=MESH)
-
     mate = p + 1 - 2 * odd
-
-    def forwarded(block):
-        at = block_rows(block)
-        return pltpu.make_async_remote_copy(
-            src_ref=dx.at[planes - odd * (planes - 1), at, :],
-            dst_ref=dx.at[(1 - odd) * (planes + 1), at, :],
-            send_sem=f_send.at[block], recv_sem=f_recv.at[block],
-            device_id=device(g, mate), device_id_type=MESH)
 
     def forward_of(block):
         at = block_rows(block)
         return pltpu.make_async_remote_copy(
             src_ref=dx.at[planes - odd * (planes - 1), at, :],
             dst_ref=dx.at[odd * (planes + 1), at, :],
-            send_sem=f_send.at[block], recv_sem=f_recv.at[block],
+            send_sem=f_send.at[0], recv_sem=f_recv.at[0],
             device_id=device(g, mate), device_id_type=MESH)
 
     for j in order:
@@ -593,35 +590,12 @@
         dx_from(j).wait_recv()
         forward_of(place(source_of(j))).start()
     own_q.wait()
-    for block in range(group):
-        forwarded(block).wait_recv()
-    for j in order:
-        q_from(j).wait_recv()
-
-    for c in range(2):
-        for j in order:
-            incoming(c, j).wait_send()
-        for k in range(0, S, 2):
-            for up in range(2):
-                @pl.when(z_there[up])
-                def _():
-                    z_copy(c, k, up).wait_send()
-
-                @pl.when(r_there[up])
-                def _():
-                    r_copy(c, k, up).wait_send()
-
-                if deep(c, k) == 2:
-                    for side in range(2):
-                        @pl.when(z_there[up] & r_there[side])
-                        def _():
-                            e_copy(c, k, up, side).wait_send()
-    pltpu.make_async_copy(others, others, a_send.at[0]).wait()
-    for j in order:
-        outgoing_dx(j).wait_send()
-        outgoing_q(j).wait_send()
-    for block in range(group):
-        forward_of(block).wait_send()
+    drained(dx.at[0], f_recv.at[0])
+    drained(others, a_send.at[0])
+    drained(out_dx.at[pl.ds(0, group - 1)], o_send.at[0])
+    drained(dx.at[0], f_send.at[0])
+    drained(last.at[:, pl.ds(0, width - rows), :], q_recv.at[0])
+    drained(last.at[:, pl.ds(0, width - rows), :], q_send.at[0])
 
 
 def finish(sol, res, dx, last, beta, sol_out, res_out, dir_out, buf, sem):
@@ -658,7 +632,7 @@
     planes, width, depth = sol.shape
     group, groups = 2 * ga, gz_count // 2
     tall, rows = planes * group, width // group
-    gram_tab, moved_tab, change_tab = (jnp.asarray(t) for t in gram_tables())
+    table = jnp.asarray(np.concatenate(gram_tables()))
     vmem = pl.BlockSpec(memory_space=pltpu.VMEM)
     dma = pltpu.SemaphoreType.DMA
     anywhere = pl.BlockSpec(memory_space=pltpu.HBM)
@@ -667,7 +641,7 @@
         functools.partial(kernel, gz_count, ga),
         out_shape=[pltpu.VMEM((planes + 2, width, depth), f32), pltpu.VMEM((planes, width, depth), f32),
                    pltpu.VMEM((8, LANES), f32)],
-        in_specs=[anywhere] * 5,
+        in_specs=[anywhere] * 3,
         out_specs=[vmem] * 3,
         scratch_shapes=[
             pltpu.VMEM((2, S + 1, tall + 4, rows, depth), f32),
@@ -681,18 +655,16 @@
             pltpu.VMEM((group, planes + 1, rows, depth), f32),
             pltpu.VMEM((group, planes + 1, rows, depth), f32),
             pltpu.VMEM((2, planes, width, depth), f32),
-            pltpu.VMEM((COUNT, SIDE, LANES), f32),
-            pltpu.VMEM((COUNT, SIDE, LANES), f32),
-            pltpu.VMEM((2, SIDE, LANES), f32),
-            dma((2, group)), dma((2, group)), dma((4,)),
-            dma((2, HALVES, 2)), dma((2, HALVES, 2)), dma((2, HALVES, 2)), dma((2, HALVES, 2)),
-            dma((2, HALVES, 2, 2)), dma((2, HALVES, 2, 2)),
+            pltpu.VMEM((2 * COUNT + 2, SIDE, LANES), f32),
+            dma((1,)), dma((2,)), dma((4,)),
+            dma((2,)), dma((2, 2, 2)), dma((2,)), dma((2, 2, 2)),
+            dma((2, 2)), dma((2, 2, 2, 2)),
             dma((1,)), dma((1,)),
-            dma((group,)), dma((group,)), dma((group,)), dma((group,)), dma((group,)), dma((group,)),
-            dma((5,)),
+            dma((1,)), dma((group,)), dma((1,)), dma((1,)), dma((1,)), dma((1,)),
+            dma((3,)),
         ],
         compiler_params=pltpu.CompilerParams(collective_id=0, has_side_effects=True, vmem_limit_bytes=VMEM_LIMIT),
-    )(*(pltpu.with_memory_space_constraint(x, pltpu.HBM) for x in (res, direction, gram_tab, moved_tab, change_tab)))
+    )(*(pltpu.with_memory_space_constraint(x, pltpu.HBM) for x in (res, direction, table)))
     shape = jax.ShapeDtypeStruct(sol.shape, f32)
     return pl.pallas_call(
         finish,

time: 62.1 us -> 60.1 us (0.968)
  Pallas kernels: 61.3 us -> 59.2 us
    pallas_call x1, Pallas kernels: 59.9 us -> 57.8 us  [on_device(): pl.pallas_call(functools.partial(kernel, gz_count, ga), out_shape=[pltpu....]
where the time goes in v2:
time: 60.1 us; the launch traced here: 59.9 us
  Pallas kernels  59.2 us (99%)
  between operations  0.67 us (1%)
    pallas_call x1, Pallas kernels, on_device(): pl.pallas_call(functools.partial(kernel, gz_count, ga), out_shape=[pltpu....  57.8 us
    pallas_call x1, Pallas kernels, on_device(): pl.pallas_call(finish, out_shape=[shape] * 3, in_specs=[vmem] * 5, out_sp...  1.45 us

profile of v2, /device:TPU:1, one launch (start us, length us, event | category | flops | bytes accessed | tf_op | source)
XLA Modules:
  0.0 59.9 jit_solution(7482218461704663164)
XLA Ops:
  0.6 0.0 copy-start
  0.6 0.0 copy-start.1
  0.7 57.8 %shard_map.67 = (f32[4,256,256]{2,1,0:T(8,128)S(1)}, f32[2,256,256]{2,1,0:T(8,128)S(1)}, f32[8,128]{1,0:T(8,128)S(1)}) custom-call(f32[2,256,256]{2,1,0:T(8,128)} %res.1, f32[2,256,256]{2,1,0:T(8,128)} %dir_ref.1, f32[98,24,128]{2,1,0:T(8,128)} %constant.2.clone.table_hbm), custom_call_target="tpu_custom_call" | custom-call | tf_op jit(solution)/shard_map/pallas_call | solution.py:640
  58.4 0.0 copy-done
  58.5 0.0 copy-done.1
  58.5 1.5 %shard_map.68 = (f32[2,256,256]{2,1,0:T(8,128)}, f32[2,256,256]{2,1,0:T(8,128)}, f32[2,256,256]{2,1,0:T(8,128)}) custom-call(f32[2,256,256]{2,1,0:T(8,128)S(1)} %copy-done.1, f32[2,256,256]{2,1,0:T(8,128)S(1)} %copy-done, f32[4,256,256]{2,1,0:T(8,128)S(1)} %get-tuple-element.6.dx, f32[2,256,256]{2,1,0:T(8,128)S(1)} %get-tuple-element.7.last, ...), custom_call_target="tpu_custom_call" | custom-call | tf_op jit(solution)/shard_map/pallas_call | solution.py:669
Async XLA Ops:
  0.6 57.8 %copy-start = (f32[2,256,256]{2,1,0:T(8,128)S(1)}, f32[2,256,256]{2,1,0:T(8,128)}, u32[]{:S(2)}) copy-start(f32[2,256,256]{2,1,0:T(8,128)} %res.1) | copy-start | bytes 1572868
  0.6 57.8 %copy-start.1 = (f32[2,256,256]{2,1,0:T(8,128)S(1)}, f32[2,256,256]{2,1,0:T(8,128)}, u32[]{:S(2)}) copy-start(f32[2,256,256]{2,1,0:T(8,128)} %sol.1) | copy-start | bytes 1572868

commit v3 on v2

--- a/solution.py
+++ b/solution.py
@@ -14,10 +14,11 @@
 next_scale = -1.0 / 3.0
 SIDE = 24
 LANES = 128
-HALVES = S // 2
-UNROLL = 12
+FIRST = (S - 2, S - 3)
+DEEP = max(FIRST)
+UNROLL = 16
 PIECES = 4
-VMEM_LIMIT = 32 * 2 ** 20
+VMEM_LIMIT = 44 * 2 ** 20
 
 
 def change_matrix(steps):
@@ -97,7 +98,7 @@
 
 def kernel(gz_count, ga, res_ref, dir_ref, table_hbm,
            dx, last, beta_ref,
-           X, halo, stage, edge, edge_in, accs, red, coef, out_dx, out_q, held, table,
+           X, halo, stage, edge, edge_in, edge_1, edge_1_in, accs, red, coef, out_dx, out_q, held, table,
            in_send, in_recv, own_sem, z_send, z_recv, r_send, r_recv, e_send, e_recv,
            a_send, a_recv, o_send, o_recv, q_send, q_recv, f_send, f_recv, load_sem):
     group = 2 * ga
@@ -138,7 +139,7 @@
     def greet(target):
         pl.semaphore_signal(barrier, inc=1, device_id=target, device_id_type=MESH)
 
-    if groups - 1 <= HALVES:
+    if groups - 1 <= 3:
         for j in range(1, group):
             greet(device(g, flipped(p, j, group)))
         for up in range(2):
@@ -164,79 +165,90 @@
         q = flipped(p, j, group)
         return pltpu.make_async_remote_copy(
             src_ref=held.at[c, :, block_rows(place(q)), :],
-            dst_ref=X.at[c, 0, pl.ds(2 + planes * p, planes)],
+            dst_ref=X.at[c, 0, pl.ds(DEEP + planes * p, planes)],
             send_sem=in_send.at[0], recv_sem=in_recv.at[c],
             device_id=device(g, q), device_id_type=MESH)
 
     def own_in(c):
         return pltpu.make_async_copy(
             held.at[c, :, block_rows(b), :],
-            X.at[c, 0, pl.ds(2 + planes * p, planes)], own_sem.at[c])
+            X.at[c, 0, pl.ds(DEEP + planes * p, planes)], own_sem.at[c])
 
     loads[0].wait()
     for j in order:
         incoming(0, j).start()
     own_in(0).start()
     loads[1].wait()
-    early = len(order) // 2 + 1
-    for j in order[:early]:
+    for j in order:
         incoming(1, j).start()
     own_in(1).start()
 
-    for side, missing, at in ((0, g == 0, 0), (1, g == groups - 1, tall + 2)):
-        @pl.when(missing)
-        def _():
-            for c in range(2):
-                for k in range(0, S, 2):
-                    X[c, k, at] = jnp.zeros((rows, depth), jnp.float32)
-                    X[c, k, at + 1] = jnp.zeros((rows, depth), jnp.float32)
-    for side, missing in ((0, b == 0), (1, b == group - 1)):
-        @pl.when(missing)
-        def _():
-            for c in range(2):
-                for k in range(0, S, 2):
-                    for d in range(2):
-                        halo[c, k, side, d] = jnp.zeros((tall, depth), jnp.float32)
-    for up in range(2):
-        for side in range(2):
-            @pl.when(jnp.logical_not(z_there[up] & r_there[side]))
+    def deep(c, k):
+        return 2 if k else FIRST[c]
+
+    def spread(c, k):
+        return 1 if k else 4 if deep(c, k) < 6 else 8
+
+    exchanges = [(c, k) for c in range(2) for k in (0, FIRST[c])]
+
+    def edges_of(c, k, incoming_side, up, side):
+        if k:
+            return (edge_1_in if incoming_side else edge_1).at[c, up, side]
+        if spread(c, k) == 4:
+            return (edge_in if incoming_side else edge).at[up, side, pl.ds(0, deep(c, k) - 1)]
+        if incoming_side:
+            return halo.at[c, k, side, pl.ds(1, deep(c, k) - 1), pl.ds(up * (tall + 8), 8)]
+        return stage.at[c, 0, side, pl.ds(0, deep(c, k) - 1), pl.ds(up * (tall - 8), 8)]
+
+    for c, k in exchanges:
+        d = deep(c, k)
+        for missing, at in ((g == 0, DEEP - d), (g == groups - 1, tall + DEEP)):
+            @pl.when(missing)
             def _():
-                for c in range(2):
-                    for h in range(HALVES):
-                        edge_in[c, h, up, side] = jnp.zeros((1, depth), jnp.float32)
-
-    def deep(c, k):
-        return 1 if c == 1 and k == S - 2 else 2
+                X[c, k, at:at + d] = jnp.zeros((d, rows, depth), jnp.float32)
+        for side, missing in ((0, b == 0), (1, b == group - 1)):
+            @pl.when(missing)
+            def _():
+                halo[c, k, side, 1:d + 1] = jnp.zeros((d, tall + 16, depth), jnp.float32)
+        for up in range(2):
+            for side in range(2):
+                @pl.when(jnp.logical_not(z_there[up] & r_there[side]))
+                def _():
+                    ref = edges_of(c, k, True, up, side)
+                    ref[...] = jnp.zeros(ref.shape, jnp.float32)
 
     def z_copy(c, k, up):
         d = deep(c, k)
-        source = 2 + tall - d if up else 2
-        target = 2 - d if up else tall + 2
+        source = DEEP + tall - d if up else DEEP
+        target = DEEP - d if up else tall + DEEP
         return pltpu.make_async_remote_copy(
             src_ref=X.at[c, k, pl.ds(source, d)],
             dst_ref=X.at[c, k, pl.ds(target, d)],
-            send_sem=z_send.at[up], recv_sem=z_recv.at[c, k // 2 % 2, up],
+            send_sem=z_send.at[up], recv_sem=z_recv.at[c, min(k, 1), up],
             device_id=device(g + 2 * up - 1, p), device_id_type=MESH)
 
     def r_copy(c, k, up):
-        return pltpu.make_async_remote_copy(
-            src_ref=stage.at[c, k // 2, up],
-            dst_ref=halo.at[c, k, 1 - up],
-            send_sem=r_send.at[up], recv_sem=r_recv.at[c, k // 2 % 2, up],
+        d = deep(c, k)
+        return pltpu.make_async_remote_copy(
+            src_ref=stage.at[c, min(k, 1), up, pl.ds(0, d)],
+            dst_ref=halo.at[c, k, 1 - up, pl.ds(1, d), pl.ds(8, tall)],
+            send_sem=r_send.at[up], recv_sem=r_recv.at[c, min(k, 1), up],
             device_id=device(g, place(b + 2 * up - 1)), device_id_type=MESH)
 
     def e_copy(c, k, up, side):
-        return pltpu.make_async_remote_copy(
-            src_ref=edge.at[c, k // 2, up, side],
-            dst_ref=edge_in.at[c, k // 2, 1 - up, 1 - side],
-            send_sem=e_send.at[up, side], recv_sem=e_recv.at[c, k // 2 % 2, 1 - up, 1 - side],
+        h = min(k, 1)
+        return pltpu.make_async_remote_copy(
+            src_ref=edges_of(c, k, False, up, side),
+            dst_ref=edges_of(c, k, True, 1 - up, 1 - side),
+            send_sem=e_send.at[c, h, up, side], recv_sem=e_recv.at[c, h, 1 - up, 1 - side],
             device_id=device(g + 2 * up - 1, place(b + 2 * side - 1)), device_id_type=MESH)
 
     def e_arrival(c, k, up, side):
-        return pltpu.make_async_remote_copy(
-            src_ref=edge.at[c, k // 2, up, side],
-            dst_ref=edge_in.at[c, k // 2, up, side],
-            send_sem=e_send.at[up, side], recv_sem=e_recv.at[c, k // 2 % 2, up, side],
+        h = min(k, 1)
+        return pltpu.make_async_remote_copy(
+            src_ref=edges_of(c, k, False, up, side),
+            dst_ref=edges_of(c, k, True, up, side),
+            send_sem=e_send.at[c, h, up, side], recv_sem=e_recv.at[c, h, up, side],
             device_id=device(g + 2 * up - 1, place(b + 2 * side - 1)), device_id_type=MESH)
 
     def send_z(c, k):
@@ -246,9 +258,17 @@
                 z_copy(c, k, up).start()
 
     def send_edges(c, k):
-        for up in range(2):
-            for side in range(2):
-                edge[c, k // 2, up, side] = X[c, k, 2 + (tall - 1) * up, (rows - 1) * side:(rows - 1) * side + 1, :]
+        n = spread(c, k)
+        if n < 8:
+            for up in range(2):
+                for side in range(2):
+                    ref = edges_of(c, k, False, up, side)
+                    for i in range(deep(c, k) - 1):
+                        if n == 1:
+                            row = (rows - 1) * side
+                            ref[i] = X[c, k, DEEP + (tall - 1) * up, row:row + 1, :]
+                        else:
+                            ref[i] = stage[c, 0, side, i, up * (tall - n):up * (tall - n) + n, :]
         for up in range(2):
             for side in range(2):
                 @pl.when(z_there[up] & r_there[side])
@@ -292,36 +312,80 @@
 
     def neighbours(cur, total, low, high, masks):
         height = cur.shape[0]
-        first_row, last_row, first_col, last_col = masks
+        first_row, last_row, _, _ = masks
         total = total + jnp.where(first_row, low, pltpu.roll(cur, 1, 0))
         total = total + jnp.where(last_row, high, pltpu.roll(cur, height - 1, 0))
+        return across_columns(cur, total, masks)
+
+    def across_columns(cur, total, masks):
+        _, _, first_col, last_col = masks
         total = total + jnp.where(first_col, 0.0, pltpu.roll(cur, 1, 1))
         return total + jnp.where(last_col, 0.0, pltpu.roll(cur, depth - 1, 1))
 
-    plane_masks, row_masks = iotas(rows), iotas(tall)
+    plane_masks, row_masks = iotas(rows), iotas(tall + 16)
     z_scale = [jnp.minimum(g, 1).astype(jnp.float32), jnp.minimum(groups - 1 - g, 1).astype(jnp.float32)]
     r_scale = [jnp.minimum(b, 1).astype(jnp.float32), jnp.minimum(group - 1 - b, 1).astype(jnp.float32)]
 
-    def extend(c, k):
+    plane_ids = lax.broadcasted_iota(jnp.int32, (tall + 16, depth), 0)
+    inside = (jnp.where(plane_ids < 8, z_scale[0], 1.0) * jnp.where(plane_ids >= tall + 8, z_scale[1], 1.0))
+
+    def settle(c, k):
+        n = spread(c, k)
+        if n < 8:
+            for up in range(2):
+                at = tall + 8 if up else 8 - n
+                for side in range(2):
+                    ref = edges_of(c, k, True, up, side)
+                    for i in range(deep(c, k) - 1):
+                        halo[c, k, side, i + 1, at:at + n, :] = ref[i]
+        for e in range(1, deep(c, k)):
+            for up in range(2):
+                at = tall - 1 + e if up else -e
+                put_row(c, k, at, X[c, k, DEEP + at])
+
+    def put_row(c, k, z, new):
+        at = pl.ds(8 + z, 1)
+        halo[c, k, 0, 0, at, :] = new[0:1]
+        halo[c, k, 1, 0, at, :] = new[rows - 1:rows]
+
+    def extend_rows(c, k, reach):
         scale = first_scale if k == 1 else next_scale
-        h = (k - 1) // 2
-        for side in range(2):
-            cur = halo[c, k - 1, side, 0]
-            total = halo[c, k - 1, side, 1] + stage[c, h, side, 0]
-            total = neighbours(cur, total, edge_in[c, h, 0, side], edge_in[c, h, 1, side], row_masks)
-            new = total * (r_scale[side] * scale)
-            if k > 1:
-                new = new - halo[c, k - 2, side, 0]
-            halo[c, k, side, 0] = new
-        for up in range(2):
-            at, out, inside = (tall + 2, tall + 3, tall + 1) if up else (1, 0, 2)
-            cur = X[c, k - 1, at]
-            total = X[c, k - 1, out] + X[c, k - 1, inside]
-            total = neighbours(cur, total, edge_in[c, h, up, 0], edge_in[c, h, up, 1], plane_masks)
-            new = total * (z_scale[up] * scale)
-            if k > 1:
-                new = new - X[c, k - 2, at]
-            X[c, k, at] = new
+
+        def extend_row(i, carry):
+            for side in range(2):
+                cur = halo[c, k - 1, side, i]
+                total = halo[c, k - 1, side, i - 1] + halo[c, k - 1, side, i + 1]
+                total = total + pltpu.roll(cur, 1, 0) + pltpu.roll(cur, tall + 15, 0)
+                total = across_columns(cur, total, row_masks)
+                new = total * (inside * (r_scale[side] * scale))
+                if k > 1:
+                    new = new - halo[c, k - 2, side, i]
+                halo[c, k, side, i] = new
+            return carry
+
+        lax.fori_loop(1, reach + 1, extend_row, 0, unroll=True)
+
+    def extend_planes(c, k, reach):
+        scale = first_scale if k == 1 else next_scale
+
+        def extend_plane(e, carry):
+            for up in range(2):
+                z = tall - 1 + e if up else -e
+                at = DEEP + z
+                cur = X[c, k - 1, at]
+                total = X[c, k - 1, at - 1] + X[c, k - 1, at + 1]
+                low = halo[c, k - 1, 0, 1, pl.ds(8 + z, 1), :]
+                high = halo[c, k - 1, 1, 1, pl.ds(8 + z, 1), :]
+                total = neighbours(cur, total, low, high, plane_masks)
+                new = total * (z_scale[up] * scale)
+                if k > 1:
+                    new = new - X[c, k - 2, at]
+                X[c, k, at] = new
+                if reach > 1:
+                    put_row(c, k, z, new)
+            return carry
+
+        lax.fori_loop(1, reach + 1, extend_plane, 0, unroll=True)
 
     def names_of(c, k):
         if c == 0:
@@ -338,37 +402,40 @@
         return names
 
     def sent(c, k):
-        return k % 2 == 0 and k < (S if c == 0 else S - 1)
-
-    def plane(c, k, z, sums):
+        return k == FIRST[c]
+
+    def plane(c, k, z, sums, reach):
         names = names_of(c, k)
-        cur = X[c, k - 1, z + 2]
-        total = X[c, k - 1, z + 1] + X[c, k - 1, z + 3]
-        low = halo[c, k - 1, 0, 0, pl.ds(z, 1), :]
-        high = halo[c, k - 1, 1, 0, pl.ds(z, 1), :]
+        at = z + DEEP
+        cur = X[c, k - 1, at]
+        total = X[c, k - 1, at - 1] + X[c, k - 1, at + 1]
+        low = halo[c, k - 1, 0, 1, pl.ds(8 + z, 1), :]
+        high = halo[c, k - 1, 1, 1, pl.ds(8 + z, 1), :]
         total = neighbours(cur, total, low, high, plane_masks)
         if k == 1:
             new = total * first_scale
         else:
-            new = total * next_scale - X[c, k - 2, z + 2]
-        X[c, k, z + 2] = new
+            new = total * next_scale - X[c, k - 2, at]
+        X[c, k, at] = new
         if sent(c, k):
             put_rows(c, k, z, new)
+        elif reach > 1:
+            put_row(c, k, z, new)
         have = {"new": new, "cur": cur}
         if any("other" in n for n in names):
-            have["other"] = X[0, k, z + 2]
+            have["other"] = X[0, k, at]
         if any("ahead" in n for n in names):
-            have["ahead"] = X[0, k + 1, z + 2]
+            have["ahead"] = X[0, k + 1, at]
         if any("start" in n for n in names):
-            have["start"] = X[0, 0, z + 2]
+            have["start"] = X[0, 0, at]
         return tuple(s + folded(have[l] * have[r]) for s, (_, l, r) in zip(sums, names))
 
     def put_rows(c, k, z, new):
+        put_row(c, k, z, new)
         at = pl.ds(z, 1)
-        stage[c, k // 2, 0, 0, at, :] = new[0:1]
-        stage[c, k // 2, 1, 0, at, :] = new[rows - 1:rows]
-        stage[c, k // 2, 0, 1, at, :] = new[1:2]
-        stage[c, k // 2, 1, 1, at, :] = new[rows - 2:rows - 1]
+        for i in range(deep(c, k)):
+            stage[c, min(k, 1), 0, i, at, :] = new[i:i + 1]
+            stage[c, min(k, 1), 1, i, at, :] = new[rows - 1 - i:rows - i]
 
     def zero_sums(c, k):
         return tuple(jnp.zeros((8, LANES), jnp.float32) for _ in names_of(c, k))
@@ -377,60 +444,60 @@
         for s, (slot, _, _) in zip(sums, names_of(c, k)):
             accs[slot] = s
 
-    def ends(c, k, width_of, sums):
+    def ends(c, k, width_of, sums, reach):
         def body(i, sums):
-            return plane(c, k, i + (i // width_of) * (tall - 2 * width_of), sums)
+            return plane(c, k, i + (i // width_of) * (tall - 2 * width_of), sums, reach)
         return lax.fori_loop(0, 2 * width_of, body, sums, unroll=True)
 
-    def middle(c, k, width_of, sums):
+    def middle(c, k, width_of, sums, reach):
         length = tall - 2 * width_of
         unroll = max(u for u in range(1, UNROLL + 1) if length % u == 0)
-        return lax.fori_loop(width_of, tall - width_of, lambda z, s: plane(c, k, z, s), sums, unroll=unroll)
+        return lax.fori_loop(width_of, tall - width_of, lambda z, s: plane(c, k, z, s, reach), sums, unroll=unroll)
 
     def chain_round(c, k):
-        a = k + 1
-        top = S if c == 0 else S - 1
-        if a == top:
-            keep(c, a, middle(c, a, 0, zero_sums(c, a)))
-            return
-        n = k + 2
-        extend(c, a)
-        sums = ends(c, a, 3, zero_sums(c, a))
-        later = ends(c, n, 2, zero_sums(c, n))
-        if sent(c, n):
-            send_z(c, n)
-            send_edges(c, n)
-        keep(c, a, middle(c, a, 3, sums))
-        later = middle(c, n, 2, later)
-        if sent(c, n):
-            send_rows(c, n)
-        keep(c, n, later)
+        d = deep(c, k)
+        settle(c, k)
+        outer = c == 1 and k == 0 and 2 * (d + 1) < tall
+        sums = []
+        for m in range(1, d + 1):
+            n, reach = k + m, d - m
+            if reach:
+                extend_rows(c, n, reach)
+                extend_planes(c, n, reach)
+            sums.append((ends if outer else middle)(c, n, 2 + reach if outer else 0, zero_sums(c, n), reach))
+        if sent(c, k + d):
+            send_z(c, k + d)
+            if outer:
+                send_edges(c, k + d)
+        for m in range(1, d + 1):
+            n, reach = k + m, d - m
+            if outer and m > 1 and reach:
+                extend_rows(c, n, reach)
+            keep(c, n, middle(c, n, 2 + reach, sums[m - 1], reach) if outer else sums[m - 1])
+        if sent(c, k + d):
+            send_rows(c, k + d)
+            if not outer:
+                send_edges(c, k + d)
 
     def arrive(c):
         own_in(c).wait()
         others = held.at[c, :, pl.ds(0, width - rows), :]
         pltpu.make_async_copy(others, others, in_recv.at[c]).wait()
         send_z(c, 0)
-        send_edges(c, 0)
 
         def copy_rows(z, carry):
-            put_rows(c, 0, z, X[c, 0, z + 2])
+            put_rows(c, 0, z, X[c, 0, z + DEEP])
             return carry
         lax.fori_loop(0, tall, copy_rows, 0, unroll=4)
+        send_edges(c, 0)
         send_rows(c, 0)
 
     arrive(0)
-    for j in order[early:]:
-        incoming(1, j).start()
-    receive(0, 0)
-    chain_round(0, 0)
     arrive(1)
-    for k in range(0, S, 2):
-        if k:
-            receive(0, k)
-            chain_round(0, k)
-        receive(1, k)
-        chain_round(1, k)
+    for h in range(2):
+        for c in range(2):
+            receive(c, h * FIRST[c])
+            chain_round(c, h * FIRST[c])
 
     lanes = lax.broadcasted_iota(jnp.int32, (8, LANES), 1)
     packed = jnp.zeros((8, LANES), jnp.float32)
@@ -457,16 +524,17 @@
     for up in range(2):
         @pl.when(z_there[up])
         def _():
-            drained(X.at[0, pl.ds(0, S // 2 + 1), pl.ds(0, 3)], z_send.at[up])
+            drained(X.at[0, pl.ds(0, 5), pl.ds(0, 3)], z_send.at[up])
 
         @pl.when(r_there[up])
         def _():
-            drained(stage.at[:, :, 0], r_send.at[up])
+            drained(halo.at[0, pl.ds(0, 3), 0, pl.ds(0, 5), pl.ds(8, tall)], r_send.at[up])
 
         for side in range(2):
             @pl.when(z_there[up] & r_there[side])
             def _():
-                drained(edge.at[:, :, 0, 0], e_send.at[up, side])
+                for c, k in exchanges:
+                    e_copy(c, k, up, side).wait_send()
     others = red.at[pl.ds(0, count - 1)]
     drained(others, a_recv.at[0])
     total = jnp.sum(red[...], axis=0)
@@ -518,7 +586,7 @@
     beta_ref[...] = jnp.zeros((8, LANES), jnp.float32) + beta
 
     def combine(q):
-        start = planes * q + 1 + q % 2
+        start = planes * q + DEEP - 1 + q % 2
 
         def strip(s, carry):
             i, part = s // (rows // 8), s % (rows // 8)
@@ -644,11 +712,13 @@
         in_specs=[anywhere] * 3,
         out_specs=[vmem] * 3,
         scratch_shapes=[
-            pltpu.VMEM((2, S + 1, tall + 4, rows, depth), f32),
-            pltpu.VMEM((2, S, 2, 2, tall, depth), f32),
-            pltpu.VMEM((2, HALVES, 2, 2, tall, depth), f32),
-            pltpu.VMEM((2, HALVES, 2, 2, 1, depth), f32),
-            pltpu.VMEM((2, HALVES, 2, 2, 1, depth), f32),
+            pltpu.VMEM((2, S + 1, tall + 2 * DEEP, rows, depth), f32),
+            pltpu.VMEM((2, S, 2, DEEP + 1, tall + 16, depth), f32),
+            pltpu.VMEM((2, 2, 2, DEEP, tall, depth), f32),
+            pltpu.VMEM((2, 2, FIRST[1] - 1, 4, depth), f32),
+            pltpu.VMEM((2, 2, FIRST[1] - 1, 4, depth), f32),
+            pltpu.VMEM((2, 2, 2, 1, 1, depth), f32),
+            pltpu.VMEM((2, 2, 2, 1, 1, depth), f32),
             pltpu.VMEM((COUNT, 8, LANES), f32),
             pltpu.VMEM((gz_count * ga, 1, LANES), f32),
             pltpu.VMEM((2, SIDE, LANES), f32),
@@ -658,7 +728,7 @@
             pltpu.VMEM((2 * COUNT + 2, SIDE, LANES), f32),
             dma((1,)), dma((2,)), dma((4,)),
             dma((2,)), dma((2, 2, 2)), dma((2,)), dma((2, 2, 2)),
-            dma((2, 2)), dma((2, 2, 2, 2)),
+            dma((2, 2, 2, 2)), dma((2, 2, 2, 2)),
             dma((1,)), dma((1,)),
             dma((1,)), dma((group,)), dma((1,)), dma((1,)), dma((1,)), dma((1,)),
             dma((3,)),

time: 60.1 us -> 56.5 us (0.940)
  Pallas kernels: 59.2 us -> 55.7 us
    pallas_call x1, Pallas kernels: 57.8 us -> 54.2 us  [on_device(): pl.pallas_call(functools.partial(kernel, gz_count, ga), out_shape=[pltpu....]
where the time goes in v3:
time: 56.5 us; the launch traced here: 56.4 us
  Pallas kernels  55.7 us (99%)
  between operations  0.67 us (1%)
    pallas_call x1, Pallas kernels, on_device(): pl.pallas_call(functools.partial(kernel, gz_count, ga), out_shape=[pltpu....  54.2 us
    pallas_call x1, Pallas kernels, on_device(): pl.pallas_call(finish, out_shape=[shape] * 3, in_specs=[vmem] * 5, out_sp...  1.45 us

profile of v3, /device:TPU:1, one launch (start us, length us, event | category | flops | bytes accessed | tf_op | source)
XLA Modules:
  0.0 56.4 jit_solution(11530055759503618259)
XLA Ops:
  0.6 0.0 copy-start
  0.6 0.0 copy-start.1
  0.7 54.2 %shard_map.67 = (f32[4,256,256]{2,1,0:T(8,128)S(1)}, f32[2,256,256]{2,1,0:T(8,128)S(1)}, f32[8,128]{1,0:T(8,128)S(1)}) custom-call(f32[2,256,256]{2,1,0:T(8,128)} %res.1, f32[2,256,256]{2,1,0:T(8,128)} %dir_ref.1, f32[98,24,128]{2,1,0:T(8,128)} %constant.2.clone.table_hbm), custom_call_target="tpu_custom_call" | custom-call | tf_op jit(solution)/shard_map/pallas_call | solution.py:708
  54.9 0.0 copy-done
  54.9 0.0 copy-done.1
  54.9 1.5 %shard_map.68 = (f32[2,256,256]{2,1,0:T(8,128)}, f32[2,256,256]{2,1,0:T(8,128)}, f32[2,256,256]{2,1,0:T(8,128)}) custom-call(f32[2,256,256]{2,1,0:T(8,128)S(1)} %copy-done.1, f32[2,256,256]{2,1,0:T(8,128)S(1)} %copy-done, f32[4,256,256]{2,1,0:T(8,128)S(1)} %get-tuple-element.6.dx, f32[2,256,256]{2,1,0:T(8,128)S(1)} %get-tuple-element.7.last, ...), custom_call_target="tpu_custom_call" | custom-call | tf_op jit(solution)/shard_map/pallas_call | solution.py:739
Async XLA Ops:
  0.6 54.3 %copy-start = (f32[2,256,256]{2,1,0:T(8,128)S(1)}, f32[2,256,256]{2,1,0:T(8,128)}, u32[]{:S(2)}) copy-start(f32[2,256,256]{2,1,0:T(8,128)} %res.1) | copy-start | bytes 1572868
  0.6 54.3 %copy-start.1 = (f32[2,256,256]{2,1,0:T(8,128)S(1)}, f32[2,256,256]{2,1,0:T(8,128)}, u32[]{:S(2)}) copy-start(f32[2,256,256]{2,1,0:T(8,128)} %sol.1) | copy-start | bytes 1572868

commit v4 on v3

--- a/solution.py
+++ b/solution.py
@@ -96,9 +96,22 @@
     return first + [j for j in range(2, group) if j not in first] + [1]
 
 
-def kernel(gz_count, ga, res_ref, dir_ref, table_hbm,
-           dx, last, beta_ref,
-           X, halo, stage, edge, edge_in, edge_1, edge_1_in, accs, red, coef, out_dx, out_q, held, table,
+def neighbours(cur, total, low, high):
+    height = cur.shape[0]
+    total = total + jnp.concatenate([low, cur[:height - 1]], axis=0)
+    total = total + jnp.concatenate([cur[1:], high], axis=0)
+    return across_columns(cur, total)
+
+
+def across_columns(cur, total):
+    none = jnp.zeros((cur.shape[0], 1), jnp.float32)
+    total = total + jnp.concatenate([none, cur[:, :cur.shape[1] - 1]], axis=1)
+    return total + jnp.concatenate([cur[:, 1:], none], axis=1)
+
+
+def kernel(gz_count, ga, res_ref, dir_ref, table_hbm, sol_ref,
+           sol_out, res_out, last, beta_ref,
+           X, halo, stage, edge, edge_in, edge_1, edge_1_in, accs, red, coef, dx, out_dx, out_q, held, sol_in, table,
            in_send, in_recv, own_sem, z_send, z_recv, r_send, r_recv, e_send, e_recv,
            a_send, a_recv, o_send, o_recv, q_send, q_recv, f_send, f_recv, load_sem):
     group = 2 * ga
@@ -126,7 +139,7 @@
         return pl.ds(pl.multiple_of(block * rows, rows), rows)
 
     loads = [pltpu.make_async_copy(source, target, load_sem.at[i]) for i, (source, target) in enumerate((
-        (dir_ref, held.at[0]), (res_ref, held.at[1]), (table_hbm, table)))]
+        (dir_ref, held.at[0]), (res_ref, held.at[1]), (table_hbm, table), (sol_ref, sol_in)))]
     for load in loads:
         load.start()
 
@@ -296,11 +309,6 @@
             def _():
                 z_copy(c, k, 1 - up).wait_recv()
 
-    def iotas(height):
-        row_ids = lax.broadcasted_iota(jnp.int32, (height, depth), 0)
-        col_ids = lax.broadcasted_iota(jnp.int32, (height, depth), 1)
-        return row_ids == 0, row_ids == height - 1, col_ids == 0, col_ids == depth - 1
-
     def folded(x):
         total = x[0:8]
         for i in range(8, rows, 8):
@@ -310,19 +318,6 @@
             out = out + total[:, i:i + LANES]
         return out
 
-    def neighbours(cur, total, low, high, masks):
-        height = cur.shape[0]
-        first_row, last_row, _, _ = masks
-        total = total + jnp.where(first_row, low, pltpu.roll(cur, 1, 0))
-        total = total + jnp.where(last_row, high, pltpu.roll(cur, height - 1, 0))
-        return across_columns(cur, total, masks)
-
-    def across_columns(cur, total, masks):
-        _, _, first_col, last_col = masks
-        total = total + jnp.where(first_col, 0.0, pltpu.roll(cur, 1, 1))
-        return total + jnp.where(last_col, 0.0, pltpu.roll(cur, depth - 1, 1))
-
-    plane_masks, row_masks = iotas(rows), iotas(tall + 16)
     z_scale = [jnp.minimum(g, 1).astype(jnp.float32), jnp.minimum(groups - 1 - g, 1).astype(jnp.float32)]
     r_scale = [jnp.minimum(b, 1).astype(jnp.float32), jnp.minimum(group - 1 - b, 1).astype(jnp.float32)]
 
@@ -356,7 +351,7 @@
                 cur = halo[c, k - 1, side, i]
                 total = halo[c, k - 1, side, i - 1] + halo[c, k - 1, side, i + 1]
                 total = total + pltpu.roll(cur, 1, 0) + pltpu.roll(cur, tall + 15, 0)
-                total = across_columns(cur, total, row_masks)
+                total = across_columns(cur, total)
                 new = total * (inside * (r_scale[side] * scale))
                 if k > 1:
                     new = new - halo[c, k - 2, side, i]
@@ -376,7 +371,7 @@
                 total = X[c, k - 1, at - 1] + X[c, k - 1, at + 1]
                 low = halo[c, k - 1, 0, 1, pl.ds(8 + z, 1), :]
                 high = halo[c, k - 1, 1, 1, pl.ds(8 + z, 1), :]
-                total = neighbours(cur, total, low, high, plane_masks)
+                total = neighbours(cur, total, low, high)
                 new = total * (z_scale[up] * scale)
                 if k > 1:
                     new = new - X[c, k - 2, at]
@@ -405,13 +400,12 @@
         return k == FIRST[c]
 
     def plane(c, k, z, sums, reach):
-        names = names_of(c, k)
         at = z + DEEP
         cur = X[c, k - 1, at]
         total = X[c, k - 1, at - 1] + X[c, k - 1, at + 1]
         low = halo[c, k - 1, 0, 1, pl.ds(8 + z, 1), :]
         high = halo[c, k - 1, 1, 1, pl.ds(8 + z, 1), :]
-        total = neighbours(cur, total, low, high, plane_masks)
+        total = neighbours(cur, total, low, high)
         if k == 1:
             new = total * first_scale
         else:
@@ -421,6 +415,11 @@
             put_rows(c, k, z, new)
         elif reach > 1:
             put_row(c, k, z, new)
+        return products(c, k, z, sums, new, cur) if sums else sums
+
+    def products(c, k, z, sums, new, cur):
+        names = names_of(c, k)
+        at = z + DEEP
         have = {"new": new, "cur": cur}
         if any("other" in n for n in names):
             have["other"] = X[0, k, at]
@@ -429,6 +428,11 @@
         if any("start" in n for n in names):
             have["start"] = X[0, 0, at]
         return tuple(s + folded(have[l] * have[r]) for s, (_, l, r) in zip(sums, names))
+
+    def all_products(c, k):
+        def body(z, sums):
+            return products(c, k, z, sums, X[c, k, z + DEEP], X[c, k - 1, z + DEEP])
+        return lax.fori_loop(0, tall, body, zero_sums(c, k), unroll=4)
 
     def put_rows(c, k, z, new):
         put_row(c, k, z, new)
@@ -464,7 +468,7 @@
             if reach:
                 extend_rows(c, n, reach)
                 extend_planes(c, n, reach)
-            sums.append((ends if outer else middle)(c, n, 2 + reach if outer else 0, zero_sums(c, n), reach))
+            sums.append((ends if outer else middle)(c, n, 2 + reach if outer else 0, () if outer else zero_sums(c, n), reach))
         if sent(c, k + d):
             send_z(c, k + d)
             if outer:
@@ -473,11 +477,17 @@
             n, reach = k + m, d - m
             if outer and m > 1 and reach:
                 extend_rows(c, n, reach)
-            keep(c, n, middle(c, n, 2 + reach, sums[m - 1], reach) if outer else sums[m - 1])
+            if outer:
+                middle(c, n, 2 + reach, (), reach)
+            else:
+                keep(c, n, sums[m - 1])
         if sent(c, k + d):
             send_rows(c, k + d)
             if not outer:
                 send_edges(c, k + d)
+        if outer:
+            for m in range(1, d + 1):
+                keep(c, k + m, all_products(c, k + m))
 
     def arrive(c):
         own_in(c).wait()
@@ -506,8 +516,10 @@
         packed = packed + jnp.where(lanes == t, part, 0.0)
     red[me] = jnp.sum(pltpu.roll(packed, 0, 1, stride=8, stride_axis=0), axis=0, keepdims=True)
 
+    far = 2 * ((2 * g) // groups) - 1
+
     def moments_to(j):
-        t = (me + j) % count
+        t = (me + far * j + count) % count
         return pltpu.make_async_remote_copy(
             src_ref=red.at[me], dst_ref=red.at[me], send_sem=a_send.at[0], recv_sem=a_recv.at[0],
             device_id=(t // ga, t % ga), device_id_type=MESH)
@@ -585,26 +597,29 @@
     coef[1] = state[0]
     beta_ref[...] = jnp.zeros((8, LANES), jnp.float32) + beta
 
-    def combine(q):
-        start = planes * q + DEEP - 1 + q % 2
-
+    tile = 16 if rows % 16 == 0 else 8
+
+    def combine(o, start, out, height):
         def strip(s, carry):
-            i, part = s // (rows // 8), s % (rows // 8)
-            at = pl.ds(pl.multiple_of(part * 8, 8), 8)
-            sums = [None, None]
+            i, part = s // (rows // tile), s % (rows // tile)
+            at = pl.ds(pl.multiple_of(part * tile, tile), tile)
+            total = None
             for v in range(2 * S - 1):
                 c, k = (0, v) if v < S else (1, v - S)
                 row = v if v < S else v + 1
-                x = X[c, k, start + i, at, :]
-                for o in range(2):
-                    f = coef[o, row:row + 1, :]
-                    f = jnp.concatenate([f] * (depth // LANES), axis=1)
-                    term = f * x
-                    sums[o] = term if sums[o] is None else sums[o] + term
-            out_dx[q, i, at, :] = sums[0]
-            out_q[q, i, at, :] = sums[1]
+                f = coef[o, row:row + 1, :]
+                f = jnp.concatenate([f] * (depth // LANES), axis=1)
+                term = f * X[c, k, start + i, at, :]
+                total = term if total is None else total + term
+            out[i, at, :] = total
             return carry
-        lax.fori_loop(0, (planes + 1) * (rows // 8), strip, 0, unroll=2)
+        lax.fori_loop(0, height * (rows // tile), strip, 0, unroll=2)
+
+    def combine_dx(q):
+        combine(0, planes * q + DEEP - 1 + q % 2, out_dx.at[q], planes + 1)
+
+    def combine_q(q):
+        combine(1, planes * q + DEEP, out_q.at[q], planes)
 
     odd = p % 2
 
@@ -618,7 +633,7 @@
     def outgoing_q(j):
         q = flipped(p, j, group)
         return pltpu.make_async_remote_copy(
-            src_ref=out_q.at[q, pl.ds(1 - q % 2, planes)], dst_ref=last.at[:, block_rows(b), :],
+            src_ref=out_q.at[q], dst_ref=last.at[:, block_rows(b), :],
             send_sem=q_send.at[0], recv_sem=q_recv.at[0],
             device_id=device(g, q), device_id_type=MESH)
 
@@ -643,14 +658,16 @@
             device_id=device(g, mate), device_id_type=MESH)
 
     for j in order:
-        combine(flipped(p, j, group))
+        combine_dx(flipped(p, j, group))
         outgoing_dx(j).start()
-    combine(p)
-    for j in order:
-        outgoing_q(j).start()
+    combine_dx(p)
     own = pltpu.make_async_copy(out_dx.at[p], dx.at[pl.ds(odd, planes + 1), block_rows(b), :], own_sem.at[2])
     own.start()
-    own_q = pltpu.make_async_copy(out_q.at[p, pl.ds(1 - odd, planes)], last.at[:, block_rows(b), :], own_sem.at[3])
+    for j in order:
+        combine_q(flipped(p, j, group))
+        outgoing_q(j).start()
+    combine_q(p)
+    own_q = pltpu.make_async_copy(out_q.at[p], last.at[:, block_rows(b), :], own_sem.at[3])
     own_q.start()
     own.wait()
     forward_of(b).start()
@@ -662,36 +679,37 @@
     drained(others, a_send.at[0])
     drained(out_dx.at[pl.ds(0, group - 1)], o_send.at[0])
     drained(dx.at[0], f_send.at[0])
+    loads[3].wait()
+
+    piece = width // PIECES
+    for i in range(planes):
+        for t in range(PIECES):
+            at = pl.ds(t * piece, piece)
+            cur = dx[i + 1, at, :]
+            none = jnp.zeros((1, depth), jnp.float32)
+            low = dx[i + 1, t * piece - 1:t * piece, :] if t else none
+            high = dx[i + 1, (t + 1) * piece:(t + 1) * piece + 1, :] if t < PIECES - 1 else none
+            total = neighbours(cur, dx[i, at, :] + dx[i + 2, at, :], low, high)
+            sol_out[i, at, :] = sol_in[i, at, :] + cur
+            res_out[i, at, :] = held[1, i, at, :] - (6.0 * cur - total)
     drained(last.at[:, pl.ds(0, width - rows), :], q_recv.at[0])
     drained(last.at[:, pl.ds(0, width - rows), :], q_send.at[0])
 
 
-def finish(sol, res, dx, last, beta, sol_out, res_out, dir_out, buf, sem):
+def finish(sol, res, last, beta, sol_out, res_out, dir_out, buf, sem):
     planes, width, depth = sol.shape
     piece = width // PIECES
-    row_ids = lax.broadcasted_iota(jnp.int32, (piece, depth), 0)
-    col_ids = lax.broadcasted_iota(jnp.int32, (piece, depth), 1)
     factor = jnp.concatenate([beta[0:1, :]] * (depth // LANES), axis=1)
-    copies = []
+    copies = [pltpu.make_async_copy(source, target, sem.at[i])
+              for i, (source, target) in enumerate(((sol, sol_out), (res, res_out)))]
+    for copy in copies:
+        copy.start()
     for i in range(planes):
         for s in range(PIECES):
             at = pl.ds(s * piece, piece)
-            cur = dx[i + 1, at, :]
-            low = dx[i + 1, s * piece - 1:s * piece, :] if s else jnp.zeros((1, depth), jnp.float32)
-            high = dx[i + 1, (s + 1) * piece:(s + 1) * piece + 1, :] if s < PIECES - 1 else jnp.zeros((1, depth), jnp.float32)
-            total = dx[i, at, :] + dx[i + 2, at, :]
-            total = total + jnp.where(row_ids == 0, low, pltpu.roll(cur, 1, 0))
-            total = total + jnp.where(row_ids == piece - 1, high, pltpu.roll(cur, piece - 1, 0))
-            total = total + jnp.where(col_ids == 0, 0.0, pltpu.roll(cur, 1, 1))
-            total = total + jnp.where(col_ids == depth - 1, 0.0, pltpu.roll(cur, depth - 1, 1))
-            buf[0, i, at, :] = sol[i, at, :] + cur
-            remain = res[i, at, :] - (6.0 * cur - total)
-            buf[1, i, at, :] = remain
-            buf[2, i, at, :] = remain + factor * last[i, at, :]
-            for o, target in enumerate((sol_out, res_out, dir_out)):
-                copy = pltpu.make_async_copy(buf.at[o, i, at, :], target.at[i, at, :], sem.at[o, i, s])
-                copy.start()
-                copies.append(copy)
+            buf[i, at, :] = res[i, at, :] + factor * last[i, at, :]
+        copies.append(pltpu.make_async_copy(buf.at[i], dir_out.at[i], sem.at[2 + i]))
+        copies[-1].start()
     for copy in copies:
         copy.wait()
 
@@ -705,12 +723,11 @@
     dma = pltpu.SemaphoreType.DMA
     anywhere = pl.BlockSpec(memory_space=pltpu.HBM)
     f32 = jnp.float32
-    dx, last, beta = pl.pallas_call(
+    outs = pl.pallas_call(
         functools.partial(kernel, gz_count, ga),
-        out_shape=[pltpu.VMEM((planes + 2, width, depth), f32), pltpu.VMEM((planes, width, depth), f32),
-                   pltpu.VMEM((8, LANES), f32)],
-        in_specs=[anywhere] * 3,
-        out_specs=[vmem] * 3,
+        out_shape=[pltpu.VMEM(sol.shape, f32)] * 3 + [pltpu.VMEM((8, LANES), f32)],
+        in_specs=[anywhere] * 4,
+        out_specs=[vmem] * 4,
         scratch_shapes=[
             pltpu.VMEM((2, S + 1, tall + 2 * DEEP, rows, depth), f32),
             pltpu.VMEM((2, S, 2, DEEP + 1, tall + 16, depth), f32),
@@ -722,28 +739,30 @@
             pltpu.VMEM((COUNT, 8, LANES), f32),
             pltpu.VMEM((gz_count * ga, 1, LANES), f32),
             pltpu.VMEM((2, SIDE, LANES), f32),
+            pltpu.VMEM((planes + 2, width, depth), f32),
             pltpu.VMEM((group, planes + 1, rows, depth), f32),
-            pltpu.VMEM((group, planes + 1, rows, depth), f32),
+            pltpu.VMEM((group, planes, rows, depth), f32),
             pltpu.VMEM((2, planes, width, depth), f32),
+            pltpu.VMEM(sol.shape, f32),
             pltpu.VMEM((2 * COUNT + 2, SIDE, LANES), f32),
             dma((1,)), dma((2,)), dma((4,)),
             dma((2,)), dma((2, 2, 2)), dma((2,)), dma((2, 2, 2)),
             dma((2, 2, 2, 2)), dma((2, 2, 2, 2)),
             dma((1,)), dma((1,)),
             dma((1,)), dma((group,)), dma((1,)), dma((1,)), dma((1,)), dma((1,)),
-            dma((3,)),
+            dma((4,)),
         ],
         compiler_params=pltpu.CompilerParams(collective_id=0, has_side_effects=True, vmem_limit_bytes=VMEM_LIMIT),
-    )(*(pltpu.with_memory_space_constraint(x, pltpu.HBM) for x in (res, direction, table)))
+    )(*(pltpu.with_memory_space_constraint(x, pltpu.HBM) for x in (res, direction, table, sol)))
     shape = jax.ShapeDtypeStruct(sol.shape, f32)
     return pl.pallas_call(
         finish,
         out_shape=[shape] * 3,
-        in_specs=[vmem] * 5,
+        in_specs=[vmem] * 4,
         out_specs=[anywhere] * 3,
-        scratch_shapes=[pltpu.VMEM((3,) + sol.shape, f32), dma((3, planes, PIECES))],
+        scratch_shapes=[pltpu.VMEM(sol.shape, f32), dma((2 + planes,))],
         compiler_params=pltpu.CompilerParams(vmem_limit_bytes=8 * 2 ** 20),
-    )(sol, res, dx, last, beta)
+    )(*outs)
 
 
 def solution(mesh):

time: 56.5 us -> 55.5 us (0.982)
  Pallas kernels: 55.7 us -> 54.7 us
    pallas_call x1, Pallas kernels: 54.2 us -> 53.5 us  [on_device(): pl.pallas_call(functools.partial(kernel, gz_count, ga), out_shape=[pltpu....]
where the time goes in v4:
time: 55.5 us; the launch traced here: 55.3 us
  Pallas kernels  54.7 us (99%)
  between operations  0.64 us (1%)
    pallas_call x1, Pallas kernels, on_device(): pl.pallas_call(functools.partial(kernel, gz_count, ga), out_shape=[pltpu....  53.5 us
    pallas_call x1, Pallas kernels, on_device(): pl.pallas_call(finish, out_shape=[shape] * 3, in_specs=[vmem] * 4, out_sp...  1.17 us

profile of v4, /device:TPU:1, one launch (start us, length us, event | category | flops | bytes accessed | tf_op | source)
XLA Modules:
  0.0 55.3 jit_solution(8901498927205082596)
XLA Ops:
  0.6 53.5 %shard_map.67 = (f32[2,256,256]{2,1,0:T(8,128)S(1)}, f32[2,256,256]{2,1,0:T(8,128)S(1)}, f32[2,256,256]{2,1,0:T(8,128)S(1)}, f32[8,128]{1,0:T(8,128)S(1)}) custom-call(f32[2,256,256]{2,1,0:T(8,128)} %res_ref.1, f32[2,256,256]{2,1,0:T(8,128)} %dir_ref.1, f32[98,24,128]{2,1,0:T(8,128)} %constant.2.clone.table_hbm, f32[2,256,256]{2,1,0:T(8,128)} %sol_ref.1), custom_call_target="tpu_custom_call" | custom-call | tf_op jit(solution)/shard_map/pallas_call | solution.py:726
  54.2 1.2 %shard_map.68 = (f32[2,256,256]{2,1,0:T(8,128)}, f32[2,256,256]{2,1,0:T(8,128)}, f32[2,256,256]{2,1,0:T(8,128)}) custom-call(f32[2,256,256]{2,1,0:T(8,128)S(1)} %get-tuple-element.7.sol, f32[2,256,256]{2,1,0:T(8,128)S(1)} %get-tuple-element.8.res, f32[2,256,256]{2,1,0:T(8,128)S(1)} %get-tuple-element.9.last, f32[8,128]{1,0:T(8,128)S(1)} %get-tuple-element.10.beta), custom_call_target="tpu_custom_call" | custom-call | tf_op jit(solution)/shard_map/pallas_call | solution.py:758

commit v5 on v4

--- a/solution.py
+++ b/solution.py
@@ -294,11 +294,13 @@
             def _():
                 r_copy(c, k, side).start()
 
-    def receive(c, k):
+    def receive_rows(c, k):
         for side in range(2):
             @pl.when(r_there[side])
             def _():
                 r_copy(c, k, 1 - side).wait_recv()
+
+    def receive_planes(c, k):
         for up in range(2):
             for side in range(2):
                 @pl.when(z_there[up] & r_there[side])
@@ -460,34 +462,39 @@
 
     def chain_round(c, k):
         d = deep(c, k)
+        outer = c == 1 and k == 0 and 2 * (d + 1) < tall
+        receive_rows(c, k)
+        inner = middle(c, k + 1, 1, () if outer else zero_sums(c, k + 1), d - 1)
+        receive_planes(c, k)
         settle(c, k)
-        outer = c == 1 and k == 0 and 2 * (d + 1) < tall
         sums = []
         for m in range(1, d + 1):
             n, reach = k + m, d - m
             if reach:
                 extend_rows(c, n, reach)
                 extend_planes(c, n, reach)
-            sums.append((ends if outer else middle)(c, n, 2 + reach if outer else 0, () if outer else zero_sums(c, n), reach))
+            if m == 1:
+                sums.append(ends(c, n, 1, inner, reach))
+            elif outer:
+                ends(c, n, 2 + reach, (), reach)
+            else:
+                sums.append(middle(c, n, 0, zero_sums(c, n), reach))
         if sent(c, k + d):
             send_z(c, k + d)
             if outer:
                 send_edges(c, k + d)
-        for m in range(1, d + 1):
-            n, reach = k + m, d - m
-            if outer and m > 1 and reach:
-                extend_rows(c, n, reach)
-            if outer:
+        if outer:
+            for m in range(2, d + 1):
+                n, reach = k + m, d - m
+                if m > 2 and reach:
+                    extend_rows(c, n, reach)
                 middle(c, n, 2 + reach, (), reach)
-            else:
-                keep(c, n, sums[m - 1])
         if sent(c, k + d):
             send_rows(c, k + d)
             if not outer:
                 send_edges(c, k + d)
-        if outer:
-            for m in range(1, d + 1):
-                keep(c, k + m, all_products(c, k + m))
+        for m in range(1, d + 1):
+            keep(c, k + m, all_products(c, k + m) if outer else sums[m - 1])
 
     def arrive(c):
         own_in(c).wait()
@@ -506,7 +513,6 @@
     arrive(1)
     for h in range(2):
         for c in range(2):
-            receive(c, h * FIRST[c])
             chain_round(c, h * FIRST[c])
 
     lanes = lax.broadcasted_iota(jnp.int32, (8, LANES), 1)

time: 55.5 us -> 55 us (level)
  no operation moved by 1% of the time
where the time goes in v5:
time: 55 us; the launch traced here: 54.9 us
  Pallas kernels  54.2 us (99%)
  between operations  0.64 us (1%)
    pallas_call x1, Pallas kernels, on_device(): pl.pallas_call(functools.partial(kernel, gz_count, ga), out_shape=[pltpu....  53 us
    pallas_call x1, Pallas kernels, on_device(): pl.pallas_call(finish, out_shape=[shape] * 3, in_specs=[vmem] * 4, out_sp...  1.17 us

profile of v5, /device:TPU:1, one launch (start us, length us, event | category | flops | bytes accessed | tf_op | source)
XLA Modules:
  0.0 54.9 jit_solution(15621701152347323953)
XLA Ops:
  0.6 53.0 %shard_map.67 = (f32[2,256,256]{2,1,0:T(8,128)S(1)}, f32[2,256,256]{2,1,0:T(8,128)S(1)}, f32[2,256,256]{2,1,0:T(8,128)S(1)}, f32[8,128]{1,0:T(8,128)S(1)}) custom-call(f32[2,256,256]{2,1,0:T(8,128)} %res_ref.1, f32[2,256,256]{2,1,0:T(8,128)} %dir_ref.1, f32[98,24,128]{2,1,0:T(8,128)} %constant.2.clone.table_hbm, f32[2,256,256]{2,1,0:T(8,128)} %sol_ref.1), custom_call_target="tpu_custom_call" | custom-call | tf_op jit(solution)/shard_map/pallas_call | solution.py:732
  53.7 1.2 %shard_map.68 = (f32[2,256,256]{2,1,0:T(8,128)}, f32[2,256,256]{2,1,0:T(8,128)}, f32[2,256,256]{2,1,0:T(8,128)}) custom-call(f32[2,256,256]{2,1,0:T(8,128)S(1)} %get-tuple-element.7.sol, f32[2,256,256]{2,1,0:T(8,128)S(1)} %get-tuple-element.8.res, f32[2,256,256]{2,1,0:T(8,128)S(1)} %get-tuple-element.9.last, f32[8,128]{1,0:T(8,128)S(1)} %get-tuple-element.10.beta), custom_call_target="tpu_custom_call" | custom-call | tf_op jit(solution)/shard_map/pallas_call | solution.py:764

commit v6 on v5

--- a/solution.py
+++ b/solution.py
@@ -111,7 +111,7 @@
 
 def kernel(gz_count, ga, res_ref, dir_ref, table_hbm, sol_ref,
            sol_out, res_out, last, beta_ref,
-           X, halo, stage, edge, edge_in, edge_1, edge_1_in, accs, red, coef, dx, out_dx, out_q, held, sol_in, table,
+           X, halo, stage, edge, edge_in, edge_0, edge_0_in, edge_1, edge_1_in, accs, red, coef, dx, out_dx, out_q, held, sol_in, table,
            in_send, in_recv, own_sem, z_send, z_recv, r_send, r_recv, e_send, e_recv,
            a_send, a_recv, o_send, o_recv, q_send, q_recv, f_send, f_recv, load_sem):
     group = 2 * ga
@@ -202,16 +202,24 @@
     def spread(c, k):
         return 1 if k else 4 if deep(c, k) < 6 else 8
 
+    def drained(ref, sem):
+        pltpu.make_async_copy(ref, ref, sem).wait()
+
     exchanges = [(c, k) for c in range(2) for k in (0, FIRST[c])]
 
-    def edges_of(c, k, incoming_side, up, side):
+    def parts(c, k):
+        return range(2 if spread(c, k) == 8 else 1)
+
+    def edges_of(c, k, incoming_side, up, side, part=0):
         if k:
             return (edge_1_in if incoming_side else edge_1).at[c, up, side]
         if spread(c, k) == 4:
             return (edge_in if incoming_side else edge).at[up, side, pl.ds(0, deep(c, k) - 1)]
+        if part:
+            return (edge_0_in if incoming_side else edge_0).at[up, side]
         if incoming_side:
-            return halo.at[c, k, side, pl.ds(1, deep(c, k) - 1), pl.ds(up * (tall + 8), 8)]
-        return stage.at[c, 0, side, pl.ds(0, deep(c, k) - 1), pl.ds(up * (tall - 8), 8)]
+            return halo.at[c, k, side, pl.ds(1, 1), pl.ds(up * (tall + 8), 8)]
+        return stage.at[c, 0, side, pl.ds(0, 1), pl.ds(up * (tall - 8), 8)]
 
     for c, k in exchanges:
         d = deep(c, k)
@@ -227,8 +235,9 @@
             for side in range(2):
                 @pl.when(jnp.logical_not(z_there[up] & r_there[side]))
                 def _():
-                    ref = edges_of(c, k, True, up, side)
-                    ref[...] = jnp.zeros(ref.shape, jnp.float32)
+                    for part in parts(c, k):
+                        ref = edges_of(c, k, True, up, side, part)
+                        ref[...] = jnp.zeros(ref.shape, jnp.float32)
 
     def z_copy(c, k, up):
         d = deep(c, k)
@@ -248,11 +257,11 @@
             send_sem=r_send.at[up], recv_sem=r_recv.at[c, min(k, 1), up],
             device_id=device(g, place(b + 2 * up - 1)), device_id_type=MESH)
 
-    def e_copy(c, k, up, side):
+    def e_copy(c, k, up, side, part=0):
         h = min(k, 1)
         return pltpu.make_async_remote_copy(
-            src_ref=edges_of(c, k, False, up, side),
-            dst_ref=edges_of(c, k, True, 1 - up, 1 - side),
+            src_ref=edges_of(c, k, False, up, side, part),
+            dst_ref=edges_of(c, k, True, 1 - up, 1 - side, part),
             send_sem=e_send.at[c, h, up, side], recv_sem=e_recv.at[c, h, 1 - up, 1 - side],
             device_id=device(g + 2 * up - 1, place(b + 2 * side - 1)), device_id_type=MESH)
 
@@ -263,6 +272,21 @@
             dst_ref=edges_of(c, k, True, up, side),
             send_sem=e_send.at[c, h, up, side], recv_sem=e_recv.at[c, h, up, side],
             device_id=device(g + 2 * up - 1, place(b + 2 * side - 1)), device_id_type=MESH)
+
+    def whole_edge(c, k):
+        return held.at[0, 0, pl.ds(0, 8 + 4 * (deep(c, k) - 2))]
+
+    def edge_arrived(c, k, up, side):
+        if spread(c, k) == 8:
+            drained(whole_edge(c, k), e_recv.at[c, min(k, 1), up, side])
+        else:
+            e_arrival(c, k, up, side).wait_recv()
+
+    def edge_left(c, k, up, side):
+        if spread(c, k) == 8:
+            drained(whole_edge(c, k), e_send.at[c, min(k, 1), up, side])
+        else:
+            e_copy(c, k, up, side).wait_send()
 
     def send_z(c, k):
         for up in range(2):
@@ -282,11 +306,17 @@
                             ref[i] = X[c, k, DEEP + (tall - 1) * up, row:row + 1, :]
                         else:
                             ref[i] = stage[c, 0, side, i, up * (tall - n):up * (tall - n) + n, :]
+        else:
+            for up in range(2):
+                for side in range(2):
+                    for i in range(1, deep(c, k) - 1):
+                        edge_0[up, side, i - 1] = stage[c, 0, side, i, up * (tall - 4):up * (tall - 4) + 4, :]
         for up in range(2):
             for side in range(2):
                 @pl.when(z_there[up] & r_there[side])
                 def _():
-                    e_copy(c, k, up, side).start()
+                    for part in parts(c, k):
+                        e_copy(c, k, up, side, part).start()
 
     def send_rows(c, k):
         for side in range(2):
@@ -305,7 +335,7 @@
             for side in range(2):
                 @pl.when(z_there[up] & r_there[side])
                 def _():
-                    e_arrival(c, k, up, side).wait_recv()
+                    edge_arrived(c, k, up, side)
 
             @pl.when(z_there[up])
             def _():
@@ -335,6 +365,12 @@
                     ref = edges_of(c, k, True, up, side)
                     for i in range(deep(c, k) - 1):
                         halo[c, k, side, i + 1, at:at + n, :] = ref[i]
+        else:
+            for up in range(2):
+                at = tall + 8 if up else 4
+                for side in range(2):
+                    for i in range(1, deep(c, k) - 1):
+                        halo[c, k, side, i + 1, at:at + 4, :] = edge_0_in[up, side, i - 1]
         for e in range(1, deep(c, k)):
             for up in range(2):
                 at = tall - 1 + e if up else -e
@@ -535,9 +571,6 @@
         return carry
 
     lax.fori_loop(1, count, start_moments, 0, unroll=count <= 64)
-    def drained(ref, sem):
-        pltpu.make_async_copy(ref, ref, sem).wait()
-
     drained(held.at[:, :, pl.ds(0, width - rows), :], in_send.at[0])
     for up in range(2):
         @pl.when(z_there[up])
@@ -552,7 +585,7 @@
             @pl.when(z_there[up] & r_there[side])
             def _():
                 for c, k in exchanges:
-                    e_copy(c, k, up, side).wait_send()
+                    edge_left(c, k, up, side)
     others = red.at[pl.ds(0, count - 1)]
     drained(others, a_recv.at[0])
     total = jnp.sum(red[...], axis=0)
@@ -740,6 +773,8 @@
             pltpu.VMEM((2, 2, 2, DEEP, tall, depth), f32),
             pltpu.VMEM((2, 2, FIRST[1] - 1, 4, depth), f32),
             pltpu.VMEM((2, 2, FIRST[1] - 1, 4, depth), f32),
+            pltpu.VMEM((2, 2, FIRST[0] - 2, 4, depth), f32),
+            pltpu.VMEM((2, 2, FIRST[0] - 2, 4, depth), f32),
             pltpu.VMEM((2, 2, 2, 1, 1, depth), f32),
             pltpu.VMEM((2, 2, 2, 1, 1, depth), f32),
             pltpu.VMEM((COUNT, 8, LANES), f32),

time: 55 us -> 54.7 us (level)
  no operation moved by 1% of the time
where the time goes in v6:
time: 54.7 us; the launch traced here: 54.5 us
  Pallas kernels  53.9 us (99%)
  between operations  0.64 us (1%)
    pallas_call x1, Pallas kernels, on_device(): pl.pallas_call(functools.partial(kernel, gz_count, ga), out_shape=[pltpu....  52.7 us
    pallas_call x1, Pallas kernels, on_device(): pl.pallas_call(finish, out_shape=[shape] * 3, in_specs=[vmem] * 4, out_sp...  1.17 us

profile of v6, /device:TPU:1, one launch (start us, length us, event | category | flops | bytes accessed | tf_op | source)
XLA Modules:
  0.0 54.5 jit_solution(6113574502715829241)
XLA Ops:
  0.6 52.7 %shard_map.67 = (f32[2,256,256]{2,1,0:T(8,128)S(1)}, f32[2,256,256]{2,1,0:T(8,128)S(1)}, f32[2,256,256]{2,1,0:T(8,128)S(1)}, f32[8,128]{1,0:T(8,128)S(1)}) custom-call(f32[2,256,256]{2,1,0:T(8,128)} %res_ref.1, f32[2,256,256]{2,1,0:T(8,128)} %dir_ref.1, f32[98,24,128]{2,1,0:T(8,128)} %constant.2.clone.table_hbm, f32[2,256,256]{2,1,0:T(8,128)} %sol_ref.1), custom_call_target="tpu_custom_call" | custom-call | tf_op jit(solution)/shard_map/pallas_call | solution.py:765
  53.4 1.2 %shard_map.68 = (f32[2,256,256]{2,1,0:T(8,128)}, f32[2,256,256]{2,1,0:T(8,128)}, f32[2,256,256]{2,1,0:T(8,128)}) custom-call(f32[2,256,256]{2,1,0:T(8,128)S(1)} %get-tuple-element.7.sol, f32[2,256,256]{2,1,0:T(8,128)S(1)} %get-tuple-element.8.res, f32[2,256,256]{2,1,0:T(8,128)S(1)} %get-tuple-element.9.last, f32[8,128]{1,0:T(8,128)S(1)} %get-tuple-element.10.beta), custom_call_target="tpu_custom_call" | custom-call | tf_op jit(solution)/shard_map/pallas_call | solution.py:799

commit v7 on v6

--- a/solution.py
+++ b/solution.py
@@ -501,6 +501,10 @@
         outer = c == 1 and k == 0 and 2 * (d + 1) < tall
         receive_rows(c, k)
         inner = middle(c, k + 1, 1, () if outer else zero_sums(c, k + 1), d - 1)
+        if outer:
+            for m in range(2, d + 1):
+                extend_rows(c, k + m - 1, d - m + 1)
+                middle(c, k + m, m, (), d - m)
         receive_planes(c, k)
         settle(c, k)
         sums = []
@@ -512,7 +516,7 @@
             if m == 1:
                 sums.append(ends(c, n, 1, inner, reach))
             elif outer:
-                ends(c, n, 2 + reach, (), reach)
+                ends(c, n, min(m, 2 + reach), (), reach)
             else:
                 sums.append(middle(c, n, 0, zero_sums(c, n), reach))
         if sent(c, k + d):
@@ -522,9 +526,9 @@
         if outer:
             for m in range(2, d + 1):
                 n, reach = k + m, d - m
-                if m > 2 and reach:
-                    extend_rows(c, n, reach)
-                middle(c, n, 2 + reach, (), reach)
+                for z in range(2 + reach, m):
+                    plane(c, n, z, (), reach)
+                    plane(c, n, tall - 1 - z, (), reach)
         if sent(c, k + d):
             send_rows(c, k + d)
             if not outer:

time: 54.7 us -> 54.6 us (level)
  no operation moved by 1% of the time
where the time goes in v7:
time: 54.6 us; the launch traced here: 54.4 us
  Pallas kernels  53.8 us (99%)
  between operations  0.64 us (1%)
    pallas_call x1, Pallas kernels, on_device(): pl.pallas_call(functools.partial(kernel, gz_count, ga), out_shape=[pltpu....  52.6 us
    pallas_call x1, Pallas kernels, on_device(): pl.pallas_call(finish, out_shape=[shape] * 3, in_specs=[vmem] * 4, out_sp...  1.17 us

profile of v7, /device:TPU:1, one launch (start us, length us, event | category | flops | bytes accessed | tf_op | source)
XLA Modules:
  0.0 54.4 jit_solution(7940496046512395419)
XLA Ops:
  0.6 52.6 %shard_map.67 = (f32[2,256,256]{2,1,0:T(8,128)S(1)}, f32[2,256,256]{2,1,0:T(8,128)S(1)}, f32[2,256,256]{2,1,0:T(8,128)S(1)}, f32[8,128]{1,0:T(8,128)S(1)}) custom-call(f32[2,256,256]{2,1,0:T(8,128)} %res_ref.1, f32[2,256,256]{2,1,0:T(8,128)} %dir_ref.1, f32[98,24,128]{2,1,0:T(8,128)} %constant.2.clone.table_hbm, f32[2,256,256]{2,1,0:T(8,128)} %sol_ref.1), custom_call_target="tpu_custom_call" | custom-call | tf_op jit(solution)/shard_map/pallas_call | solution.py:769
  53.2 1.2 %shard_map.68 = (f32[2,256,256]{2,1,0:T(8,128)}, f32[2,256,256]{2,1,0:T(8,128)}, f32[2,256,256]{2,1,0:T(8,128)}) custom-call(f32[2,256,256]{2,1,0:T(8,128)S(1)} %get-tuple-element.7.sol, f32[2,256,256]{2,1,0:T(8,128)S(1)} %get-tuple-element.8.res, f32[2,256,256]{2,1,0:T(8,128)S(1)} %get-tuple-element.9.last, f32[8,128]{1,0:T(8,128)S(1)} %get-tuple-element.10.beta), custom_call_target="tpu_custom_call" | custom-call | tf_op jit(solution)/shard_map/pallas_call | solution.py:803
